TPU v7x, 32 devices: a 4x2x2 block of a 4x4x8 slice. The times are simulated.
32 devices in a mesh: dp: 4 (over y, z), sp: 8 (over x, core).
Axes of the slice: x: 4, y: 2, z: 2, core: 2. Of those that a mesh axis runs over, the one named last changes fastest.
The devices are a block of a 4x4x8 slice.
Arguments:
- latent: bfloat16 [64, 8, 192, 640], P('dp', 'sp'), parts along dimension 0
- time_emb: bfloat16 [64, 1280], P('dp'), parts along dimension 0
- context: bfloat16 [64, 77, 768], P('dp'), parts along dimension 0
- res_conv: bfloat16 [2, 2, 3, 3, 640, 640], replicated
- res_time: bfloat16 [2, 1280, 640], replicated
- res_norm: bfloat16 [2, 2, 2, 32, 20], replicated
- attn_norm: bfloat16 [2, 32, 20], replicated
- proj_inout: bfloat16 [2, 640, 640], replicated
- self_qkv: bfloat16 [3, 640, 8, 80], replicated
- self_out: bfloat16 [8, 80, 640], replicated
- cross_q: bfloat16 [640, 8, 80], replicated
- cross_kv: bfloat16 [2, 768, 8, 80], replicated
- cross_out: bfloat16 [8, 80, 640], replicated
- ff_in: bfloat16 [640, 5120], replicated
- ff_out: bfloat16 [2560, 640], replicated
Outputs:
- output: bfloat16 [64, 8, 192, 640], P('dp', 'sp'), parts along dimension 0
There are 4 independent parts. A program takes and returns all parts, laid end to end along the dimension named above; an argument that names none is the same for every part.
All inputs are finite; a program needn't handle non-finite values.
Results may differ from a plain program's by a relative error of at most 0.0135156.
Values are sent between devices in bfloat16 or wider.
A program may use at most 768 MiB of HBM per device.

v0:
```python
import jax
import jax.numpy as jnp
from jax import lax
from jax.sharding import PartitionSpec as P

GN_EPS = 1e-6
LN_EPS = 1e-5


def group_norm(hidden, scale_shift, elem_count):
    groups = scale_shift.shape[1]
    feat_f32 = hidden.astype(jnp.float32).reshape(hidden.shape[:-1] + (groups, -1))
    local_sums = jnp.stack([jnp.sum(feat_f32, axis=(1, 2, 4)), jnp.sum(feat_f32 * feat_f32, axis=(1, 2, 4))])
    stat_sums = lax.psum(local_sums, 'sp')
    grp_mean = stat_sums[0] / elem_count
    grp_rstd = lax.rsqrt(stat_sums[1] / elem_count - grp_mean * grp_mean + GN_EPS)
    normed = (feat_f32 - grp_mean[:, None, None, :, None]) * grp_rstd[:, None, None, :, None]
    normed = normed * scale_shift[0].astype(jnp.float32) + scale_shift[1].astype(jnp.float32)
    return normed.reshape(hidden.shape)


def conv_band(act_in, kernel, num_bands):
    to_next = [(source, source + 1) for source in range(num_bands - 1)]
    to_prev = [(source + 1, source) for source in range(num_bands - 1)]
    top_halo = lax.ppermute(act_in[:, -1:], 'sp', to_next)
    bottom_halo = lax.ppermute(act_in[:, :1], 'sp', to_prev)
    padded = jnp.concatenate([top_halo, act_in, bottom_halo], axis=1)
    return lax.conv_general_dilated(padded, kernel, (1, 1), ((0, 0), (1, 1)), dimension_numbers=('NHWC', 'HWIO', 'NHWC'), preferred_element_type=jnp.float32)


def time_project(time_emb, weight):
    time_act = jax.nn.silu(time_emb.astype(jnp.float32)).astype(jnp.bfloat16)
    return jnp.dot(time_act, weight, preferred_element_type=jnp.float32)


def res_block(hidden, time_proj, kernels, norm_pair, elem_count, num_bands):
    act_one = jax.nn.silu(group_norm(hidden, norm_pair[0], elem_count)).astype(jnp.bfloat16)
    mid_act = (conv_band(act_one, kernels[0], num_bands) + time_proj[:, None, None, :]).astype(jnp.bfloat16)
    act_two = jax.nn.silu(group_norm(mid_act, norm_pair[1], elem_count)).astype(jnp.bfloat16)
    return (hidden.astype(jnp.float32) + conv_band(act_two, kernels[1], num_bands)).astype(jnp.bfloat16)


def layer_norm(tokens):
    feat_f32 = tokens.astype(jnp.float32)
    centred = feat_f32 - jnp.mean(feat_f32, axis=-1, keepdims=True)
    return (centred * lax.rsqrt(jnp.mean(centred * centred, axis=-1, keepdims=True) + LN_EPS)).astype(jnp.bfloat16)


def project(rows_flat, weight):
    return jnp.einsum('tc,chd->thd', rows_flat, weight, preferred_element_type=jnp.float32).astype(jnp.bfloat16)


def attend(queries, key_all, val_all):
    logit_scale = queries.shape[-1] ** -0.5
    logits = jnp.einsum('bqhd,bkhd->bhqk', queries, key_all, preferred_element_type=jnp.float32) * logit_scale
    row_max = jnp.max(logits, axis=-1, keepdims=True)
    weights = jnp.exp(logits - row_max)
    row_sum = jnp.sum(weights, axis=-1, keepdims=True)
    weighted = jnp.einsum('bhqk,bkhd->bhqd', weights.astype(jnp.bfloat16), val_all, preferred_element_type=jnp.float32)
    return (weighted / row_sum).astype(jnp.bfloat16)


def out_project(attended, weight):
    return jnp.einsum('bhqd,hdc->bqc', attended, weight, preferred_element_type=jnp.float32)


def transformer(hidden, context, attn_norm, proj_inout, self_qkv, self_out, cross_q, cross_kv, cross_out, ff_in, ff_out, elem_count):
    batch_size, band_rows, img_width, channels = hidden.shape
    band_shape = (batch_size, band_rows * img_width, self_qkv.shape[2], self_qkv.shape[3])
    row_count = batch_size * band_rows * img_width
    normed = group_norm(hidden, attn_norm, elem_count).astype(jnp.bfloat16).reshape(row_count, channels)
    tokens = jnp.dot(normed, proj_inout[0], preferred_element_type=jnp.float32).astype(jnp.bfloat16)
    ln_tokens = layer_norm(tokens)
    key_all = lax.all_gather(project(ln_tokens, self_qkv[1]).reshape(band_shape), 'sp', axis=1, tiled=True)
    val_all = lax.all_gather(project(ln_tokens, self_qkv[2]).reshape(band_shape), 'sp', axis=1, tiled=True)
    self_query = project(ln_tokens, self_qkv[0]).reshape(band_shape)
    self_att = out_project(attend(self_query, key_all, val_all), self_out).reshape(row_count, channels)
    tok_one = (tokens.astype(jnp.float32) + self_att).astype(jnp.bfloat16)
    ctx_key = jnp.einsum('btc,chd->bthd', context, cross_kv[0], preferred_element_type=jnp.float32).astype(jnp.bfloat16)
    ctx_val = jnp.einsum('btc,chd->bthd', context, cross_kv[1], preferred_element_type=jnp.float32).astype(jnp.bfloat16)
    cross_query = project(layer_norm(tok_one), cross_q).reshape(band_shape)
    cross_att = out_project(attend(cross_query, ctx_key, ctx_val), cross_out).reshape(row_count, channels)
    tok_two = (tok_one.astype(jnp.float32) + cross_att).astype(jnp.bfloat16)
    hidden_ff = jnp.dot(layer_norm(tok_two), ff_in, preferred_element_type=jnp.float32)
    ff_width = ff_out.shape[0]
    gated_ff = (hidden_ff[:, :ff_width] * jax.nn.gelu(hidden_ff[:, ff_width:], approximate=False)).astype(jnp.bfloat16)
    tok_three = (tok_two.astype(jnp.float32) + jnp.dot(gated_ff, ff_out, preferred_element_type=jnp.float32)).astype(jnp.bfloat16)
    block_out = hidden.reshape(row_count, channels).astype(jnp.float32) + jnp.dot(tok_three, proj_inout[1], preferred_element_type=jnp.float32)
    return block_out.astype(jnp.bfloat16).reshape(hidden.shape)


def solution(mesh):
    num_bands = mesh.shape['sp']

    def local_stage(latent, time_emb, context, res_conv, res_time, res_norm, attn_norm, proj_inout, self_qkv, self_out, cross_q, cross_kv, cross_out, ff_in, ff_out):
        elem_count = float(latent.shape[1] * num_bands * latent.shape[2] * res_norm.shape[4])
        first_out = res_block(latent, time_project(time_emb, res_time[0]), res_conv[0], res_norm[0], elem_count, num_bands)
        middle = transformer(first_out, context, attn_norm, proj_inout, self_qkv, self_out, cross_q, cross_kv, cross_out, ff_in, ff_out, elem_count)
        return res_block(middle, time_project(time_emb, res_time[1]), res_conv[1], res_norm[1], elem_count, num_bands)

    band_spec = P('dp', 'sp', None, None)
    shared = P()
    in_specs = (band_spec, P('dp', None), P('dp', None, None)) + (shared,) * 12
    return jax.shard_map(local_stage, mesh=mesh, in_specs=in_specs, out_specs=band_spec, check_vma=False)
```

profile of v0, /device:TPU:81, one launch (start us, length us, event | category | flops | bytes accessed | tf_op | source)
XLA Modules:
  0.0 1322.6 jit_solution(9758530188629849847)
XLA Ops:
  6.6 4.9 convert_reduce_fusion
  15.5 24.0 %psum.35 = f32[2,16,32]{2,1,0:T(8,128)S(1)} all-reduce(f32[2,16,32]{2,1,0:T(8,128)S(1)} %pad_maximum_fusion), channel_id=1, replica_groups=mesh['dp'=4,'sp'=8] {'sp'}, use_global_device_ids=true, to_apply=%region_4.5 | all-reduce | flops 1024 | bytes 8192 | tf_op jit(solution)/shard_map/psum | solution.py:14
  46.5 6.6 fusion.92
  56.7 5.3 collective-permute-start.1
  64.7 34.5 %collective-permute-done = bf16[16,1,192,640]{3,0,2,1:T(8,128)(2,1)} collective-permute-done((bf16[16,1,192,640]{3,0,2,1:T(8,128)(2,1)}, bf16[16,1,192,640]{3,0,2,1:T(8,128)(2,1)}, u32[]{:S(2)}, u32[]{:S(2)}) %collective-permute-start) | collective-permute-done | bytes 3932192 | tf_op jit(solution)/shard_map/ppermute | solution.py:25
  99.3 4.4 collective-permute-done.1
  103.7 34.2 %convert_reduce_fusion.5 = (f32[16,640]{1,0:T(8,128)}, f32[16,640]{1,0:T(8,128)}, bf16[16,1,192,640]{3,0,2,1:T(8,128)(2,1)}) fusion(f32[16,640]{1,0:T(8,128)S(1)} %fusion.170, bf16[2,2,3,3,640,640]{5,4,3,2,1,0:T(8,128)(2,1)} %param.18, bf16[16,1,192,640]{3,0,2,1:T(8,128)(2,1)} %collective-permute-done.1, bf16[16,1,192,640]{3,0,2,1:T(8,128)(2,1)} %fusion.92, ...), kind=kOutput, calls=%fused_computation.73 | convolution fusion | flops 22617763840 | bytes 23224320 | tf_op jit(solution)/shard_map/conv_general_dilated | solution.py:28
  142.2 20.4 %psum.36 = f32[2,16,32]{2,1,0:T(8,128)S(1)} all-reduce(f32[2,16,32]{2,1,0:T(8,128)S(1)} %pad_maximum_fusion.1), channel_id=1, replica_groups=mesh['dp'=4,'sp'=8] {'sp'}, use_global_device_ids=true, to_apply=%region_9.10 | all-reduce | flops 1024 | bytes 8192 | tf_op jit(solution)/shard_map/psum | solution.py:14
  165.8 6.0 fusion.69
  175.4 5.2 collective-permute-start.3
  184.8 33.1 %collective-permute-done.2 = bf16[16,1,192,640]{3,0,2,1:T(8,128)(2,1)} collective-permute-done((bf16[16,1,192,640]{3,0,2,1:T(8,128)(2,1)}, bf16[16,1,192,640]{3,0,2,1:T(8,128)(2,1)}, u32[]{:S(2)}, u32[]{:S(2)}) %collective-permute-start.2) | collective-permute-done | bytes 3932192 | tf_op jit(solution)/shard_map/ppermute | solution.py:25
  217.9 4.4 collective-permute-done.3
  222.4 37.6 %convert_reduce_fusion.6 = (f32[16,640]{1,0:T(8,128)}, f32[16,640]{1,0:T(8,128)}, bf16[16,1,192,640]{3,0,2,1:T(8,128)(2,1)}) fusion(bf16[2,2,3,3,640,640]{5,4,3,2,1,0:T(8,128)(2,1)} %param.18, bf16[16,1,192,640]{3,0,2,1:T(8,128)(2,1)} %collective-permute-done.3, bf16[16,1,192,640]{3,0,2,1:T(8,128)(2,1)} %fusion.69, ...), kind=kOutput, calls=%fused_computation.143 | convolution fusion | flops 22619729920 | bytes 27115520 | tf_op jit(solution)/shard_map/conv_general_dilated | solution.py:28
  264.4 20.9 %psum.37 = f32[2,16,32]{2,1,0:T(8,128)S(1)} all-reduce(f32[2,16,32]{2,1,0:T(8,128)S(1)} %pad_maximum_fusion.2), channel_id=1, replica_groups=mesh['dp'=4,'sp'=8] {'sp'}, use_global_device_ids=true, to_apply=%region_14.15 | all-reduce | flops 1024 | bytes 8192 | tf_op jit(solution)/shard_map/psum | solution.py:14
  303.6 9.7 reshape.505
  313.3 16.6 %copy.146 = bf16[16,192,8,80]{3,2,0,1:T(8,128)(2,1)} copy(bf16[16,192,8,80]{1,0,3,2:T(8,128)(2,1)} %reshape.505) | data formatting | bytes 7864320 | tf_op jit(solution)/shard_map/reshape | solution.py:74
  330.0 5.6 fusion.163
  338.1 9.9 reshape.506
  348.0 16.5 %copy.150 = bf16[16,192,8,80]{3,2,0,1:T(8,128)(2,1)} copy(bf16[16,192,8,80]{1,0,3,2:T(8,128)(2,1)} %reshape.506) | data formatting | bytes 7864320 | tf_op jit(solution)/shard_map/reshape | solution.py:75
  368.4 5.4 convolution_convert_fusion.1
  383.8 9.7 reshape.504
  393.5 165.4 %all-gather.3.cloned.1.call-done = bf16[16,1536,8,80]{3,2,0,1:T(8,128)(2,1)} async-done(((bf16[16,192,8,80]{3,2,0,1:T(8,128)(2,1)}), bf16[16,1536,8,80]{3,2,0,1:T(8,128)(2,1)}) %all-gather.3.cloned.1.call-update) | async-done | bytes 31457296 | tf_op jit(solution)/shard_map/all_gather | solution.py:74
  558.9 104.2 %multiply_reduce_fusion = (f32[16,8,192]{2,1,0:T(8,128)S(1)}, f32[16,8,192,1536]{3,2,1,0:T(8,128)}) fusion(bf16[16,1536,8,80]{3,2,0,1:T(8,128)(2,1)} %all-gather.3.cloned.1.call-done, bf16[16,192,8,80]{1,0,3,2:T(8,128)(2,1)} %reshape.504), kind=kOutput, calls=%fused_computation.1 | convolution fusion | flops 6115270656 | bytes 186482688 | tf_op jit(solution)/shard_map/bqhd,bkhd->bhqk/dot_general | solution.py:55
  663.1 46.1 %fusion = f32[16,8,192]{2,1,0:T(8,128)S(1)} fusion(f32[16,8,192,1536]{3,2,1,0:T(8,128)} %get-tuple-element.37, f32[16,8,192]{2,1,0:T(8,128)S(1)} %get-tuple-element.36), kind=kLoop, calls=%fused_computation.2 | loop fusion | flops 113221632 | bytes 151191552 | tf_op jit(solution)/shard_map/reduce_sum | solution.py:58
  709.2 75.9 %all-gather.5.cloned.1.call-done = bf16[16,1536,8,80]{3,2,0,1:T(8,128)(2,1)} async-done(((bf16[16,192,8,80]{3,2,0,1:T(8,128)(2,1)}), bf16[16,1536,8,80]{3,2,0,1:T(8,128)(2,1)}) %all-gather.5.cloned.1.call-update) | async-done | bytes 31457296 | tf_op jit(solution)/shard_map/all_gather | solution.py:75
  785.0 66.3 %fusion.120 = f32[16,192,640,1]{2,1,3,0:T(8,128)} fusion(bf16[16,1536,8,80]{3,2,0,1:T(8,128)(2,1)} %all-gather.5.cloned.1.call-done, f32[16,8,192,1536]{3,2,1,0:T(8,128)} %get-tuple-element.37, f32[16,8,192]{2,1,0:T(8,128)S(1)} %get-tuple-element.36, f32[16,8,192]{2,1,0:T(8,128)S(1)} %fusion, bf16[8,80,640]{2,1,0:T(8,128)(2,1)} %param.24), kind=kOutput, calls=%fused_computation.153 | convolution fusion | flops 8673558528 | bytes 191332352 | tf_op jit(solution)/shard_map/bhqd,hdc->bqc/dot_general | solution.py:64
  851.4 9.2 copy.152
  860.6 5.9 convert_reduce_fusion.3
  873.4 9.7 reshape.508
  883.1 11.0 multiply_reduce_fusion.2
  894.1 6.9 fusion.52
  901.0 14.5 %fusion.116 = f32[16,192,640,1]{2,1,3,0:T(8,128)} fusion(f32[16,8,192]{2,1,0:T(8,128)S(1)} %fusion.52, f32[16,8,192,77]{2,3,1,0:T(8,128)} %get-tuple-element.39, f32[16,8,192]{2,1,0:T(8,128)S(1)} %get-tuple-element.38, bf16[16,77,8,80]{3,0,2,1:T(8,128)(2,1)} %convolution_convert_fusion.1, bf16[8,80,640]{2,1,0:T(8,128)(2,1)} %param.27), kind=kOutput, calls=%fused_computation.150 | convolution fusion | flops 2828967936 | bytes 18026496 | tf_op jit(solution)/shard_map/bhqd,hdc->bqc/dot_general | solution.py:64
  915.5 9.1 copy.157
  924.6 5.8 convert_reduce_fusion.2
  933.4 35.9 %fusion.125 = f32[3072,5120]{1,0:T(8,128)} fusion(bf16[640,5120]{1,0:T(8,128)(2,1)} %param.28, bf16[3072,640]{0,1:T(8,128)(2,1)} %copy-done.6, f32[3072]{0:T(1024)S(1)} %add_rsqrt_fusion, f32[3072]{0:T(1024)S(1)} %broadcast_multiply_fusion), kind=kOutput, calls=%fused_computation.155 | convolution fusion | flops 20140523520 | bytes 73424896 | tf_op jit(solution)/shard_map/dot_general | solution.py:84
  969.3 88.0 %fusion.117 = f32[3072,640]{1,0:T(8,128)} fusion(f32[16,1,192,640]{3,2,0,1:T(8,128)} %copy.138, bf16[3072,640]{0,1:T(8,128)(2,1)} %copy-done.6, bf16[2560,640]{1,0:T(8,128)(2,1)S(1)} %copy-done, f32[3072,5120]{1,0:T(8,128)} %fusion.125, bf16[640,640]{1,0:T(8,128)(2,1)} %fusion.318), kind=kOutput, calls=%fused_computation.151 | convolution fusion | flops 13113753600 | bytes 86671360 | tf_op jit(solution)/shard_map/dot_general | solution.py:88
  1057.3 9.1 copy.159
  1066.4 11.0 reshape.518
  1077.4 5.6 fusion.287
  1083.1 20.9 %psum.38 = f32[2,16,32]{2,1,0:T(8,128)S(1)} all-reduce(f32[2,16,32]{2,1,0:T(8,128)S(1)} %pad_maximum_fusion.3), channel_id=1, replica_groups=mesh['dp'=4,'sp'=8] {'sp'}, use_global_device_ids=true, to_apply=%region_27.28 | all-reduce | flops 1024 | bytes 8192 | tf_op jit(solution)/shard_map/psum | solution.py:14
  1104.6 10.2 multiply_convert_fusion
  1118.4 5.0 collective-permute-start.5
  1125.7 35.4 %collective-permute-done.4 = bf16[16,1,192,640]{3,0,2,1:T(8,128)(2,1)} collective-permute-done((bf16[16,1,192,640]{3,0,2,1:T(8,128)(2,1)}, bf16[16,1,192,640]{3,0,2,1:T(8,128)(2,1)}, u32[]{:S(2)}, u32[]{:S(2)}) %collective-permute-start.4) | collective-permute-done | bytes 3932192 | tf_op jit(solution)/shard_map/ppermute | solution.py:25
  1161.0 4.4 collective-permute-done.5
  1165.5 34.1 %convert_reduce_fusion.1 = (f32[16,640]{1,0:T(8,128)S(1)}, f32[16,640]{1,0:T(8,128)S(1)}, bf16[16,1,192,640]{3,0,2,1:T(8,128)(2,1)}) fusion(f32[16,640]{1,0:T(8,128)S(1)} %fusion.168, bf16[2,2,3,3,640,640]{5,4,3,2,1,0:T(8,128)(2,1)} %param.18, bf16[16,1,192,640]{3,0,2,1:T(8,128)(2,1)} %collective-permute-done.5, ...), kind=kOutput, calls=%fused_computation.61 | convolution fusion | flops 22617763840 | bytes 23224320 | tf_op jit(solution)/shard_map/conv_general_dilated | solution.py:28
  1200.4 20.4 %psum.39 = f32[2,16,32]{2,1,0:T(8,128)S(1)} all-reduce(f32[2,16,32]{2,1,0:T(8,128)S(1)} %pad_maximum_fusion.4), channel_id=1, replica_groups=mesh['dp'=4,'sp'=8] {'sp'}, use_global_device_ids=true, to_apply=%region_32.33 | all-reduce | flops 1024 | bytes 8192 | tf_op jit(solution)/shard_map/psum | solution.py:14
  1232.8 39.2 %collective-permute-done.6 = bf16[16,1,192,640]{3,0,2,1:T(8,128)(2,1)S(1)} collective-permute-done((bf16[16,1,192,640]{3,0,2,1:T(8,128)(2,1)S(1)}, bf16[16,1,192,640]{3,0,2,1:T(8,128)(2,1)S(1)}, u32[]{:S(2)}, u32[]{:S(2)}) %collective-permute-start.6) | collective-permute-done | bytes 3932192 | tf_op jit(solution)/shard_map/ppermute | solution.py:25
  1276.5 36.3 %add_convert_fusion = bf16[16,1,192,640]{3,0,2,1:T(8,128)(2,1)S(1)} fusion(f32[16,1,192,640]{3,2,0,1:T(8,128)} %bitcast.208, bf16[2,2,3,3,640,640]{5,4,3,2,1,0:T(8,128)(2,1)} %param.18, bf16[16,1,192,640]{3,0,2,1:T(8,128)(2,1)S(1)} %collective-permute-done.7, bf16[16,1,192,640]{3,0,2,1:T(8,128)(2,1)S(1)} %fusion.82, ...), kind=kOutput, calls=%fused_computation.129 | convolution fusion | flops 22609920000 | bytes 30965760 | tf_op jit(solution)/shard_map/conv_general_dilated | solution.py:28
  (158 shorter events, 107.8 us)
Async XLA Ops:
  6.5 962.7 %copy-start = (bf16[2560,640]{1,0:T(8,128)(2,1)S(1)}, bf16[2560,640]{1,0:T(8,128)(2,1)}, u32[]{:S(2)}) copy-start(bf16[2560,640]{1,0:T(8,128)(2,1)} %param.29) | copy-start | bytes 9830404
  6.6 552.3 %all-gather.3.cloned.1.call-start = ((), (), s32[]{:S(2)}) async-start(), calls=%async_computation | async-start | bytes 56623104 | tf_op jit(solution)/shard_map/all_gather | solution.py:74
  46.5 15.5 %copy-start.13 = (bf16[1,1,1,32,20]{3,2,4,1,0:T(2,128)(2,1)S(1)}, bf16[1,1,1,32,20]{3,2,4,1,0:T(2,128)(2,1)}, u32[]{:S(2)}) copy-start(bf16[1,1,1,32,20]{3,2,4,1,0:T(2,128)(2,1)} %get-tuple-element.25) | copy-start | bytes 3844
  46.5 15.5 %copy-start.14 = (bf16[1,1,1,32,20]{3,2,4,1,0:T(2,128)(2,1)S(1)}, bf16[1,1,1,32,20]{3,2,4,1,0:T(2,128)(2,1)}, u32[]{:S(2)}) copy-start(bf16[1,1,1,32,20]{3,2,4,1,0:T(2,128)(2,1)} %get-tuple-element.26) | copy-start | bytes 3844
  46.5 16.5 %copy-start.19 = (bf16[16,1280]{1,0:T(8,128)(2,1)S(1)}, bf16[16,1280]{1,0:T(8,128)(2,1)}, u32[]{:S(2)}) copy-start(bf16[16,1280]{1,0:T(8,128)(2,1)} %param.16) | copy-start | bytes 122884
  53.1 46.2 %collective-permute-start = (bf16[16,1,192,640]{3,0,2,1:T(8,128)(2,1)}, bf16[16,1,192,640]{3,0,2,1:T(8,128)(2,1)}, u32[]{:S(2)}, u32[]{:S(2)}) collective-permute-start(bf16[16,1,192,640]{3,0,2,1:T(8,128)(2,1)} %fusion.92), channel_id=1, source_target_pairs={{0,1},{1,2},{2,3},{3,4},{4,5},{5,6},{6,7},{8,9},{9,10},{10,11},{11... | collective-permute-start | bytes 11796488 | tf_op jit(solution)/shard_map/ppermute | solution.py:25
  56.7 47.0 %collective-permute-start.1 = (bf16[16,1,192,640]{3,0,2,1:T(8,128)(2,1)}, bf16[16,1,192,640]{3,0,2,1:T(8,128)(2,1)}, u32[]{:S(2)}, u32[]{:S(2)}) collective-permute-start(bf16[16,1,192,640]{3,0,2,1:T(8,128)(2,1)} %fusion.92), channel_id=1, source_target_pairs={{1,0},{2,1},{3,2},{4,3},{5,4},{6,5},{7,6},{9,8},{10,9},{11,10},{12... | collective-permute-start | bytes 11796488 | tf_op jit(solution)/shard_map/ppermute | solution.py:26
  165.8 14.9 %copy-start.15 = (bf16[2,32,20]{1,0,2:T(2,128)(2,1)S(1)}, bf16[2,32,20]{1,0,2:T(2,128)(2,1)}, u32[]{:S(2)}) copy-start(bf16[2,32,20]{1,0,2:T(2,128)(2,1)} %param.21) | copy-start | bytes 7684
  171.7 46.2 %collective-permute-start.2 = (bf16[16,1,192,640]{3,0,2,1:T(8,128)(2,1)}, bf16[16,1,192,640]{3,0,2,1:T(8,128)(2,1)}, u32[]{:S(2)}, u32[]{:S(2)}) collective-permute-start(bf16[16,1,192,640]{3,0,2,1:T(8,128)(2,1)} %fusion.69), channel_id=1, source_target_pairs={{0,1},{1,2},{2,3},{3,4},{4,5},{5,6},{6,7},{8,9},{9,10},{10,11},{11... | collective-permute-start | bytes 11796488 | tf_op jit(solution)/shard_map/ppermute | solution.py:25
  175.4 47.0 %collective-permute-start.3 = (bf16[16,1,192,640]{3,0,2,1:T(8,128)(2,1)}, bf16[16,1,192,640]{3,0,2,1:T(8,128)(2,1)}, u32[]{:S(2)}, u32[]{:S(2)}) collective-permute-start(bf16[16,1,192,640]{3,0,2,1:T(8,128)(2,1)} %fusion.69), channel_id=1, source_target_pairs={{1,0},{2,1},{3,2},{4,3},{5,4},{6,5},{7,6},{9,8},{10,9},{11,10},{12... | collective-permute-start | bytes 11796488 | tf_op jit(solution)/shard_map/ppermute | solution.py:26
  288.4 4.6 copy-start.9
  293.1 4.7 copy-start.8
  296.7 4.4 copy-start.4
  329.9 455.1 %all-gather.5.cloned.1.call-start = ((), (), s32[]{:S(2)}) async-start(), calls=%async_computation.1 | async-start | bytes 56623104 | tf_op jit(solution)/shard_map/all_gather | solution.py:75
  348.0 16.6 %copy-start.12 = (bf16[1,1,1,32,20]{3,2,4,1,0:T(2,128)(2,1)S(1)}, bf16[1,1,1,32,20]{3,2,4,1,0:T(2,128)(2,1)}, u32[]{:S(2)}) copy-start(bf16[1,1,1,32,20]{3,2,4,1,0:T(2,128)(2,1)} %get-tuple-element.24) | copy-start | bytes 3844
  366.2 7.7 copy-start.3
  373.9 4.1 copy-start.5
  373.9 4.1 copy-start.7
  860.6 7.0 copy-start.18
  866.5 4.4 copy-start.2
  930.4 1.9 copy-start.6
  1077.4 27.2 %copy-start.16 = (f32[640]{0:T(1024)S(1)}, f32[640]{0:T(1024)}, u32[]{:S(2)}) copy-start(f32[640]{0:T(1024)} %reshape.519) | copy-start | bytes 7684
  1077.4 27.2 %copy-start.17 = (f32[640]{0:T(1024)S(1)}, f32[640]{0:T(1024)}, u32[]{:S(2)}) copy-start(f32[640]{0:T(1024)} %reshape.520) | copy-start | bytes 7684
  1083.0 40.5 %copy-start.10 = (bf16[1,1,1,32,20]{3,2,4,1,0:T(2,128)(2,1)S(1)}, bf16[1,1,1,32,20]{3,2,4,1,0:T(2,128)(2,1)}, u32[]{:S(2)}) copy-start(bf16[1,1,1,32,20]{3,2,4,1,0:T(2,128)(2,1)} %get-tuple-element.22) | copy-start | bytes 3844
  1083.0 40.5 %copy-start.11 = (bf16[1,1,1,32,20]{3,2,4,1,0:T(2,128)(2,1)S(1)}, bf16[1,1,1,32,20]{3,2,4,1,0:T(2,128)(2,1)}, u32[]{:S(2)}) copy-start(bf16[1,1,1,32,20]{3,2,4,1,0:T(2,128)(2,1)} %get-tuple-element.29) | copy-start | bytes 3844
  1083.0 40.9 %copy-start.20 = (bf16[16,1280]{1,0:T(8,128)(2,1)S(1)}, bf16[16,1280]{1,0:T(8,128)(2,1)}, u32[]{:S(2)}) copy-start(bf16[16,1280]{1,0:T(8,128)(2,1)} %param.16) | copy-start | bytes 122884
  1114.8 46.2 %collective-permute-start.4 = (bf16[16,1,192,640]{3,0,2,1:T(8,128)(2,1)}, bf16[16,1,192,640]{3,0,2,1:T(8,128)(2,1)}, u32[]{:S(2)}, u32[]{:S(2)}) collective-permute-start(bf16[16,1,192,640]{3,0,2,1:T(8,128)(2,1)} %multiply_convert_fusion), channel_id=1, source_target_pairs={{0,1},{1,2},{2,3},{3,4},{4,5},{5,6},{6,7},{8,9},{9,10},{10,11},{11... | collective-permute-start | bytes 11796488 | tf_op jit(solution)/shard_map/ppermute | solution.py:25
  1118.4 47.0 %collective-permute-start.5 = (bf16[16,1,192,640]{3,0,2,1:T(8,128)(2,1)}, bf16[16,1,192,640]{3,0,2,1:T(8,128)(2,1)}, u32[]{:S(2)}, u32[]{:S(2)}) collective-permute-start(bf16[16,1,192,640]{3,0,2,1:T(8,128)(2,1)} %multiply_convert_fusion), channel_id=1, source_target_pairs={{1,0},{2,1},{3,2},{4,3},{5,4},{6,5},{7,6},{9,8},{10,9},{11,10},{12... | collective-permute-start | bytes 11796488 | tf_op jit(solution)/shard_map/ppermute | solution.py:26
  1225.8 46.2 %collective-permute-start.6 = (bf16[16,1,192,640]{3,0,2,1:T(8,128)(2,1)S(1)}, bf16[16,1,192,640]{3,0,2,1:T(8,128)(2,1)S(1)}, u32[]{:S(2)}, u32[]{:S(2)}) collective-permute-start(bf16[16,1,192,640]{3,0,2,1:T(8,128)(2,1)S(1)} %fusion.82), channel_id=1, source_target_pairs={{0,1},{1,2},{2,3},{3,4},{4,5},{5,6},{6,7},{8,9},{9,10},{10,11},{11... | collective-permute-start | bytes 11796488 | tf_op jit(solution)/shard_map/ppermute | solution.py:25
  1229.4 47.0 %collective-permute-start.7 = (bf16[16,1,192,640]{3,0,2,1:T(8,128)(2,1)S(1)}, bf16[16,1,192,640]{3,0,2,1:T(8,128)(2,1)S(1)}, u32[]{:S(2)}, u32[]{:S(2)}) collective-permute-start(bf16[16,1,192,640]{3,0,2,1:T(8,128)(2,1)S(1)} %fusion.82), channel_id=1, source_target_pairs={{1,0},{2,1},{3,2},{4,3},{5,4},{6,5},{7,6},{9,8},{10,9},{11,10},{12... | collective-permute-start | bytes 11796488 | tf_op jit(solution)/shard_map/ppermute | solution.py:26
  1276.5 39.1 %copy-start.1 = (bf16[2560,640]{1,0:T(8,128)(2,1)S(1)}, bf16[2560,640]{1,0:T(8,128)(2,1)}, u32[]{:S(2)}) copy-start(bf16[2560,640]{1,0:T(8,128)(2,1)} %param.29) | copy-start | bytes 9830404
Sparse Core Ops, SparseCore 0:
  330.0 228.8 all-gather.2
  560.5 224.5 all-gather.4
where the time goes:
time: 1330 us; the launch traced here: 1320 us
  matrix products  490 us (37%)
  waiting for transfers between devices  401 us (30%)
  local copies, waits for them, and re-layouts  149 us (11%)
  other arithmetic  128 us (10%)
  blocking collectives  107 us (8%)
  starting transfers between devices  33.6 us (3%)
  between operations  14.3 us (1%)
    all_gather x1, waiting for transfers between devices, transformer(): lax.all_gather(project(ln_tokens, self_qkv[1]).reshape(band_shape), 'sp',...  165 us
    ppermute x4, waiting for transfers between devices, conv_band(): top_halo = lax.ppermute(act_in[:, -1:], 'sp', to_next)  142 us
    conv_general_dilated x4, matrix products, conv_band(): lax.conv_general_dilated(padded, kernel, (1, 1), ((0, 0), (1, 1)), dimens...  142 us
    dot_general x2, matrix products, attend(): jnp.einsum('bqhd,bkhd->bhqk', queries, key_all, preferred_element_type=jn...  115 us
    psum x5, blocking collectives, group_norm(): stat_sums = lax.psum(local_sums, 'sp')  107 us
    dot_general x1, matrix products, transformer(): jnp.dot(tok_three, proj_inout[1], preferred_element_type=jnp.float32)  88 us
    dot_general x2, matrix products, out_project(): jnp.einsum('bhqd,hdc->bqc', attended, weight, preferred_element_type=jnp....  80.9 us
    all_gather x1, waiting for transfers between devices, transformer(): lax.all_gather(project(ln_tokens, self_qkv[2]).reshape(band_shape), 'sp',...  75.9 us
  transfers between devices with their start and end apart: 10, of which 10 were waited for; matrix products, arithmetic and copies ran while one was open for 17% of the time, Pallas kernels for 0%

commit v1 on v0

v1 whole, which is shorter than its diff:
```python
import functools
import math
import jax
import jax.numpy as jnp
from jax import lax
from jax.experimental import pallas as pl
from jax.experimental.pallas import tpu as pltpu
from jax.sharding import PartitionSpec as P

GN_EPS = 1e-6
LN_EPS = 1e-5
LANES = 128
SUBLANES = 8
MESH = pl.DeviceIdType.MESH
LOGIT_LIMIT = 60.0
VALUE_LIMIT = 1e8
MIB = 2 ** 20
F32 = jnp.float32
BF16 = jnp.bfloat16
LHS_T = (((0,), (0,)), ((), ()))
BOTH_T = (((0,), (1,)), ((), ()))


def tdot(weight, act):
    return lax.dot_general(weight, act, LHS_T, preferred_element_type=F32)


def lane_sum(parts, value):
    total = parts
    for off in range(0, value.shape[1], LANES):
        total = total + value[:, off:off + LANES]
    return total


def group_affine(sums, squares, width, count, gain, shift):
    span = math.lcm(width, SUBLANES)
    row = lax.broadcasted_iota(jnp.int32, (SUBLANES, LANES), 0)
    scales, offsets = [], []

    def group_mean(array, base, low, high):
        total = None
        for top in range(0, span, SUBLANES):
            first, last = max(low - top, 0), min(high - top, SUBLANES)
            if first < last:
                tile = array[base + top:base + top + SUBLANES]
                if last - first < SUBLANES:
                    tile = jnp.where((row >= first) & (row < last), tile, 0.0)
                total = tile if total is None else total + tile
        for turn in (4, 2, 1):
            total = total + pltpu.roll(total, turn, 0)
        return jnp.broadcast_to(jnp.sum(total, axis=1, keepdims=True), (SUBLANES, LANES)) / count

    for base in range(0, sums.shape[0], span):
        means, rstds = [], []
        for low in range(0, span, width):
            mean = group_mean(sums, base, low, low + width)
            means.append(mean)
            rstds.append(lax.rsqrt(group_mean(squares, base, low, low + width) - mean * mean + GN_EPS))
        for top in range(0, span, SUBLANES):
            mean, rstd = means[top // width], rstds[top // width]
            for nxt in range(top // width + 1, (top + SUBLANES - 1) // width + 1):
                mean = jnp.where(row >= nxt * width - top, means[nxt], mean)
                rstd = jnp.where(row >= nxt * width - top, rstds[nxt], rstd)
            here = slice(base + top, base + top + SUBLANES)
            scale = rstd * gain[here]
            scales.append(scale)
            offsets.append(shift[here] - mean * scale)
    return jnp.concatenate(scales, axis=0), jnp.concatenate(offsets, axis=0)


def affine(block, scale, offset):
    pieces = [block[:, off:off + LANES].astype(F32) * scale + offset for off in range(0, block.shape[1], LANES)]
    return jnp.concatenate(pieces, axis=1)


def silu(value):
    half = 0.5 * value
    return half + half * jnp.tanh(half)


def layer_norm(tokens):
    centred = tokens - jnp.mean(tokens, axis=0, keepdims=True)
    return (centred * lax.rsqrt(jnp.mean(centred * centred, axis=0, keepdims=True) + LN_EPS)).astype(BF16)


def res_phase(which, first, width, group_width, hid, cols, cur, wide, aff, weight, sums, squares, conv_block, turn, emit):
    channels, tokens = cur.shape
    count = float(tokens * group_width)
    gain = jnp.where(first, cols[:, 0:1], cols[:, 2:3])
    shift = jnp.where(first, cols[:, 1:2], cols[:, 3:4])
    aff[0], aff[1] = group_affine(sums, squares, group_width, count, gain, shift)
    act_block = 2 * width
    row = lax.broadcasted_iota(jnp.int32, (act_block, channels), 0)
    row = jnp.where(row >= width, row - width, row)

    def widen(i, carry):
        tok = pl.ds(pl.multiple_of(i * act_block, LANES), act_block)
        act = silu(affine(cur[:, tok], aff[0], aff[1])).T
        dst = pl.ds(pl.multiple_of(i * act_block + width, 64), act_block)
        wide[dst, 0:channels] = jnp.where(row == 0, 0.0, pltpu.roll(act, 1, 0)).astype(BF16)
        wide[dst, channels:2 * channels] = act.astype(BF16)
        wide[dst, 2 * channels:3 * channels] = jnp.where(row == width - 1, 0.0, pltpu.roll(act, act_block - 1, 0)).astype(BF16)
        return carry

    lax.fori_loop(0, tokens // act_block, widen, 0)
    if weight[1] is not None:
        weight[1].wait()
    time_term = cols[:, 4:5]

    def convolve(i, carry):
        block = lax.rem(i + turn, tokens // conv_block)
        start = block * conv_block
        tok = pl.ds(pl.multiple_of(start, LANES), conv_block)
        taps_in = jnp.concatenate([wide[pl.ds(pl.multiple_of(start + dy * width, 64), conv_block), :] for dy in range(3)], axis=1)
        value = lax.dot_general(weight[0][which], taps_in, BOTH_T, preferred_element_type=F32)
        out = value + jnp.where(first, time_term, hid[:, tok].astype(F32))
        cur[:, tok] = out.astype(BF16)
        emit(block, tok, out)
        out = out.astype(BF16).astype(F32)
        return lane_sum(carry[0], out), lane_sum(carry[1], out * out)

    zero = jnp.zeros((channels, LANES), F32)
    return lax.fori_loop(0, tokens // conv_block, convolve, (zero, zero))


def clear_border(wide, width):
    rows, taps = wide.shape
    wide[0:width, :] = jnp.zeros((width, taps), BF16)
    wide[rows - width:rows, :] = jnp.zeros((width, taps), BF16)


def weight_copies(weight_hbm, weight_scr, sems, first_conv):
    return lambda i: pltpu.make_async_copy(weight_hbm.at[first_conv + i], weight_scr.at[i], sems.at[i])


def res_in_kernel(width, group_width, first_conv, conv_block, hid_ref, cols_ref, weight_hbm, *refs):
    out_ref, parts_ref, hid_scr, wide_scr, aff_scr, weight_scr, sems = refs[-7:]
    channels, tokens = hid_scr.shape
    copies = weight_copies(weight_hbm, weight_scr, sems, first_conv)
    for i in range(2):
        copies(i).start()
    clear_border(wide_scr, width)
    act_block = 2 * width
    cur = out_ref.at[0]

    def load(i, carry):
        tok = pl.ds(pl.multiple_of(i * act_block, LANES), act_block)
        block = hid_ref[tok, :].astype(F32).T
        hid_scr[:, tok] = block.astype(BF16)
        cur[:, tok] = block.astype(BF16)
        return lane_sum(carry[0], block), lane_sum(carry[1], block * block)

    zero = jnp.zeros((channels, LANES), F32)
    stats = lax.fori_loop(0, tokens // act_block, load, (zero, zero))

    def half(which, stats):
        return res_phase(which, which == 0, width, group_width, hid_scr, cols_ref[0], cur, wide_scr, aff_scr, (weight_scr, copies(which)), *stats, conv_block, 0, lambda block, tok, out: None)

    sums, squares = lax.fori_loop(0, 2, half, stats)
    parts_ref[0, :, 0:LANES] = sums
    parts_ref[0, :, LANES:2 * LANES] = squares


def res_out_kernel(axis, bands, width, group_width, first_conv, conv_block, hid_ref, parts_ref, cols_ref, weight_hbm, out_hbm, cur_scr, wide_scr, aff_scr, rows_scr, weight_scr, sems, send_sems, recv_sems, own_sems):
    images, channels, tokens = hid_ref.shape
    band = tokens // bands
    me = lax.axis_index(axis)
    copies = weight_copies(weight_hbm, weight_scr, sems, first_conv)
    for i in range(2):
        copies(i).start()
    barrier = pltpu.get_barrier_semaphore()
    for step in range(1, bands):
        pl.semaphore_signal(barrier, inc=1, device_id={axis: lax.rem(me + step, bands)}, device_id_type=MESH)
    clear_border(wide_scr, width)
    pl.semaphore_wait(barrier, bands - 1)

    turn = lax.div(me * band, conv_block) + 1

    def remote(image, peer, source, low=0, high=band):
        return pltpu.make_async_remote_copy(
            src_ref=rows_scr.at[image, pl.ds(peer * band + low, high - low)], dst_ref=out_hbm.at[image * bands + source, pl.ds(low, high - low)],
            send_sem=send_sems.at[image, peer], recv_sem=recv_sems.at[image, source], device_id={axis: peer}, device_id_type=MESH)

    def local(image, peer, low=0, high=band):
        return pltpu.make_async_copy(rows_scr.at[image, pl.ds(peer * band + low, high - low)], out_hbm.at[image * bands + me, pl.ds(low, high - low)], own_sems.at[image])

    def per_image(image, carry):
        cur_scr[...] = hid_ref[image]

        def half(which, stats):
            def emit(block, tok, out):
                rows_scr[image, tok, :] = out.T.astype(BF16)
                for ready in range(tokens // conv_block):
                    for peer in range(bands):
                        low = max(ready * conv_block - peer * band, 0)
                        high = min((ready + 1) * conv_block - peer * band, band)
                        if low >= high:
                            continue
                        now = (which == 1) & (block == ready)

                        @pl.when(now & (me != peer))
                        def _():
                            remote(image, peer, me, low, high).start()

                        @pl.when(now & (me == peer))
                        def _():
                            local(image, peer, low, high).start()

            @pl.when((image == 0))
            def _():
                copies(which).wait()

            return res_phase(which, which == 0, width, group_width, hid_ref.at[image], cols_ref[image], cur_scr, wide_scr, aff_scr, (weight_scr, None), *stats, conv_block, turn, emit)

        lax.fori_loop(0, 2, half, (parts_ref[image, :, 0:LANES], parts_ref[image, :, LANES:2 * LANES]))
        return carry

    lax.fori_loop(0, images, per_image, 0)
    for image in range(images):
        for peer in range(bands):
            @pl.when(me != peer)
            def _():
                remote(image, peer, me).wait_send()
                remote(image, peer, peer).wait_recv()
        local(image, me).wait()


def res_cost(images, channels, tokens):
    return pl.CostEstimate(flops=2 * 2 * 9 * images * channels * channels * tokens, bytes_accessed=40 * channels * channels, transcendentals=0)


def res_block_in(image, images, hid, cols, weights, first_conv, width, group_width, before):
    tokens, channels = hid.shape
    conv_block, taps = 512, 3 * channels
    slot = lambda i: (image, 0, 0)
    any_spec = pl.BlockSpec(memory_space=pl.ANY)
    return pl.pallas_call(
        functools.partial(res_in_kernel, width, group_width, first_conv, conv_block),
        grid=(1,),
        out_shape=(jax.ShapeDtypeStruct((images, channels, tokens), BF16), jax.ShapeDtypeStruct((images, channels, 2 * LANES), F32)),
        in_specs=[pl.BlockSpec(hid.shape, lambda i: (0, 0)), pl.BlockSpec((1,) + cols.shape[1:], slot), pl.BlockSpec(memory_space=pltpu.HBM)] + [any_spec] * len(before),
        out_specs=(pl.BlockSpec((1, channels, tokens), slot), pl.BlockSpec((1, channels, 2 * LANES), slot)),
        scratch_shapes=[
            pltpu.VMEM((channels, tokens), BF16), pltpu.VMEM((tokens + 2 * width, taps), BF16),
            pltpu.VMEM((2, channels, LANES), F32), pltpu.VMEM((2, 3 * taps, channels), BF16), pltpu.SemaphoreType.DMA((2,))],
        input_output_aliases={3: 0, 4: 1} if before else {},
        name='res_in',
        cost_estimate=res_cost(1, channels, tokens),
        compiler_params=pltpu.CompilerParams(vmem_limit_bytes=62 * MIB),
    )(hid, cols, weights, *before)


def res_block_out(axis, bands, stacked, parts, cols, weights, first_conv, width, group_width):
    images, channels, tokens = stacked.shape
    conv_block, taps = 512, 3 * channels
    vmem = pl.BlockSpec(memory_space=pltpu.VMEM)
    return pl.pallas_call(
        functools.partial(res_out_kernel, axis, bands, width, group_width, first_conv, conv_block),
        out_shape=jax.ShapeDtypeStruct((images * bands, tokens // bands, channels), BF16),
        in_specs=[vmem, vmem, vmem, pl.BlockSpec(memory_space=pltpu.HBM)],
        out_specs=pl.BlockSpec(memory_space=pltpu.HBM),
        scratch_shapes=[
            pltpu.VMEM((channels, tokens), BF16), pltpu.VMEM((tokens + 2 * width, taps), BF16),
            pltpu.VMEM((2, channels, LANES), F32), pltpu.VMEM((images, tokens, channels), BF16), pltpu.VMEM((2, 3 * taps, channels), BF16),
            pltpu.SemaphoreType.DMA((2,)), pltpu.SemaphoreType.DMA((images, bands)), pltpu.SemaphoreType.DMA((images, bands)), pltpu.SemaphoreType.DMA((images,))],
        name='res_out',
        cost_estimate=res_cost(images, channels, tokens),
        compiler_params=pltpu.CompilerParams(vmem_limit_bytes=48 * MIB, collective_id=0, has_side_effects=True),
    )(stacked, parts, cols, weights)


def former_kernel(heads, text, group_width, block, q_block, k_chunk, hid_ref, part_in_ref, cols_ref, ctx_key_ref, ctx_val_ref, *refs):
    weights_hbm, refs = refs[:8], refs[8:]
    out_ref, parts_ref, tok_scr, query_scr, key_scr, val_scr, att_scr, logit_scr, prob_scr, cross_scr, gate_scr = refs[:11]
    weights, sems = refs[11:19], refs[19]
    _, channels, tokens = hid_ref.shape
    head_dim = channels // heads
    ff_width = weights[6].shape[0]
    count = float(tokens * group_width)
    exp_scale = head_dim ** -0.5 * 1.4426950408889634
    first = pl.program_id(0) == 0
    copies = [pltpu.make_async_copy(weights_hbm[i], weights[i], sems.at[i]) for i in range(8)]

    @pl.when(first)
    def _():
        for copy in copies:
            copy.start()
        query_scr[...] = jnp.zeros(query_scr.shape, BF16)

    def ready(*which):
        @pl.when(first)
        def _():
            for i in which:
                copies[i].wait()

    scale, offset = group_affine(part_in_ref[0, :, 0:LANES], part_in_ref[0, :, LANES:2 * LANES], group_width, count, cols_ref[:, 0:1], cols_ref[:, 1:2])
    ready(0, 1)
    pad = jnp.zeros((query_scr.shape[1] - head_dim, block), BF16)

    def largest(value, before):
        square = value.astype(F32)
        square = (square * square).reshape(heads, head_dim, block)
        return jnp.maximum(jnp.sum(square, axis=1), before)

    def project(i, carry):
        tok = pl.ds(pl.multiple_of(i * block, LANES), block)
        token = tdot(weights[0][...], affine(hid_ref[0, :, tok], scale, offset).astype(BF16)).astype(BF16)
        tok_scr[:, tok] = token
        normed = layer_norm(token.astype(F32))
        query = tdot(weights[1][0], normed).astype(BF16)
        key = tdot(weights[1][1], normed).astype(BF16)
        value = tdot(weights[1][2], normed).astype(BF16)
        val_scr[:, tok] = value
        for h in range(heads):
            query_scr[h, 0:head_dim, tok] = query[h * head_dim:(h + 1) * head_dim]
            key_scr[h, tok, :] = jnp.concatenate([key[h * head_dim:(h + 1) * head_dim], pad], axis=0).T
        return largest(query, carry[0]), largest(key, carry[1]), largest(value, carry[2])

    zero = jnp.zeros((heads, block), F32)
    norms = lax.fori_loop(0, tokens // block, project, (zero, zero, zero))
    query_norm, key_norm, value_norm = [jnp.max(norm, axis=1, keepdims=True) for norm in norms]
    logit_bound = jnp.max(query_norm * key_norm) / head_dim
    small = (logit_bound <= LOGIT_LIMIT ** 2) & (jnp.max(value_norm) <= VALUE_LIMIT ** 2)
    blocks, chunks = tokens // q_block, tokens // k_chunk

    def fold(combine, part):
        return combine(part.reshape(k_chunk // SUBLANES, SUBLANES, q_block), axis=0)

    def logits(h, cols, c):
        return jnp.dot(key_scr[h, c * k_chunk:(c + 1) * k_chunk, :], query_scr[h, :, cols], preferred_element_type=F32)

    def weigh(h, cols, slot, total):
        head = pl.ds(pl.multiple_of(h * head_dim, 16), head_dim)
        mixed = jnp.dot(val_scr[head, :], prob_scr[slot], preferred_element_type=F32)
        att_scr[head, cols] = (mixed * (1.0 / total)).astype(BF16)

    def attend(h, last_total):
        for b in range(blocks):
            cols = slice(b * q_block, (b + 1) * q_block)
            total = 0.0
            for c in range(chunks):
                prob = jnp.exp2(logits(h, cols, c) * exp_scale)
                total = total + fold(jnp.sum, prob)
                prob_scr[b % 2, c * k_chunk:(c + 1) * k_chunk, :] = prob.astype(BF16)
                if c == 1:
                    done = (b - 1) % blocks
                    weigh(h if b else jnp.maximum(h - 1, 0), slice(done * q_block, (done + 1) * q_block), done % 2, last_total)
            last_total = jnp.sum(total, axis=0, keepdims=True)
        return last_total

    @pl.when(small)
    def _():
        prob_scr[(blocks - 1) % 2] = jnp.zeros(prob_scr.shape[1:], BF16)
        total = lax.fori_loop(0, heads, attend, jnp.ones((1, q_block), F32))
        weigh(heads - 1, slice((blocks - 1) * q_block, blocks * q_block), (blocks - 1) % 2, total)

    @pl.when(jnp.logical_not(small))
    def _():
        def attend_shifted(i, carry):
            h = lax.div(i, blocks)
            cols = pl.ds(pl.multiple_of(lax.rem(i, blocks) * q_block, LANES), q_block)
            peak = None
            for c in range(chunks):
                part = logits(h, cols, c)
                logit_scr[c * k_chunk:(c + 1) * k_chunk, :] = part
                peak = fold(jnp.max, part) if peak is None else jnp.maximum(peak, fold(jnp.max, part))
            peak = jnp.max(peak, axis=0, keepdims=True)
            total = 0.0
            for c in range(chunks):
                prob = jnp.exp2((logit_scr[c * k_chunk:(c + 1) * k_chunk, :] - peak) * exp_scale)
                total = total + fold(jnp.sum, prob)
                prob_scr[0, c * k_chunk:(c + 1) * k_chunk, :] = prob.astype(BF16)
            weigh(h, cols, 0, jnp.sum(total, axis=0, keepdims=True))
            return carry

        lax.fori_loop(0, heads * blocks, attend_shifted, 0)

    ready(2, 3, 4, 5, 6, 7)
    text_pad = ctx_key_ref.shape[2]
    text_row = lax.broadcasted_iota(jnp.int32, (text_pad, block), 0)
    cross_pad = jnp.zeros((LANES - text_pad, block), BF16)

    def finish(i, carry):
        tok = pl.ds(pl.multiple_of(i * block, LANES), block)
        tok_one = (tok_scr[:, tok].astype(F32) + tdot(weights[2][...], att_scr[:, tok])).astype(BF16)
        query = tdot(weights[3][...], layer_norm(tok_one.astype(F32))).astype(BF16)
        for h in range(heads):
            head = slice(h * head_dim, (h + 1) * head_dim)
            logit = jnp.dot(ctx_key_ref[0, h], jnp.concatenate([query[head], pad], axis=0), preferred_element_type=F32)
            logit = jnp.where(text_row < text, logit, -jnp.inf)
            prob = jnp.exp2((logit - jnp.max(logit, axis=0, keepdims=True)) * exp_scale)
            total = jnp.sum(prob, axis=0, keepdims=True)
            mixed = jnp.dot(ctx_val_ref[0, head, :], jnp.concatenate([prob.astype(BF16), cross_pad], axis=0), preferred_element_type=F32)
            cross_scr[head, :] = (mixed * (1.0 / total)).astype(BF16)
        tok_two = (tok_one.astype(F32) + tdot(weights[4][...], cross_scr[...])).astype(BF16)
        normed = layer_norm(tok_two.astype(F32))
        chunk = channels
        for off in range(0, ff_width, chunk):
            value = tdot(weights[5][:, off:off + chunk], normed)
            gate = tdot(weights[5][:, ff_width + off:ff_width + off + chunk], normed)
            gate_scr[off:off + chunk, :] = (value * (0.5 * gate * (1.0 + lax.erf(gate * (0.5 ** 0.5))))).astype(BF16)
        tok_three = (tok_two.astype(F32) + tdot(weights[6][...], gate_scr[...])).astype(BF16)
        out = (hid_ref[0, :, tok].astype(F32) + tdot(weights[7][...], tok_three)).astype(BF16)
        out_ref[0, :, tok] = out
        out = out.astype(F32)
        return lane_sum(carry[0], out), lane_sum(carry[1], out * out)

    zero = jnp.zeros((channels, LANES), F32)
    sums, squares = lax.fori_loop(0, tokens // block, finish, (zero, zero))
    parts_ref[0, :, 0:LANES] = sums
    parts_ref[0, :, LANES:2 * LANES] = squares


def former(stacked, parts, cols, ctx_key, ctx_val, weights, text, group_width):
    images, channels, tokens = stacked.shape
    heads = ctx_key.shape[1]
    block, q_block, k_chunk = 512, 256, 256
    per_image = lambda a: pl.BlockSpec((1,) + a.shape[1:], lambda i: (i,) + (0,) * (a.ndim - 1))
    whole = lambda a: pl.BlockSpec(a.shape, lambda i: (0,) * a.ndim)
    ff_width = weights[6].shape[0]
    flops = 2 * images * tokens * (channels * channels * 8 + 3 * channels * ff_width + 2 * tokens * channels * 3)
    return pl.pallas_call(
        functools.partial(former_kernel, heads, text, group_width, block, q_block, k_chunk),
        grid=(images,),
        out_shape=(jax.ShapeDtypeStruct(stacked.shape, BF16), jax.ShapeDtypeStruct(parts.shape, F32)),
        in_specs=[per_image(stacked), per_image(parts), whole(cols), per_image(ctx_key), per_image(ctx_val)] + [pl.BlockSpec(memory_space=pltpu.HBM)] * len(weights),
        out_specs=(per_image(stacked), per_image(parts)),
        scratch_shapes=[
            pltpu.VMEM((channels, tokens), BF16), pltpu.VMEM((heads, LANES, tokens), BF16), pltpu.VMEM((heads, tokens, LANES), BF16),
            pltpu.VMEM((channels, tokens), BF16), pltpu.VMEM((channels, tokens), BF16),
            pltpu.VMEM((tokens, q_block), F32), pltpu.VMEM((2, tokens, q_block), BF16),
            pltpu.VMEM((channels, block), BF16), pltpu.VMEM((ff_width, block), BF16)]
        + [pltpu.VMEM(w.shape, BF16) for w in weights] + [pltpu.SemaphoreType.DMA((len(weights),))],
        name='former',
        cost_estimate=pl.CostEstimate(flops=flops, bytes_accessed=60 * MIB, transcendentals=0),
        compiler_params=pltpu.CompilerParams(vmem_limit_bytes=60 * MIB),
    )(stacked, parts, cols, ctx_key, ctx_val, *weights)


def time_project(time_emb, weight):
    time_act = jax.nn.silu(time_emb.astype(F32)).astype(BF16)
    return jnp.dot(time_act, weight, preferred_element_type=F32)


def solution(mesh):
    num_bands = mesh.shape['sp']

    def local_stage(latent, time_emb, context, res_conv, res_time, res_norm, attn_norm, proj_inout, self_qkv, self_out, cross_q, cross_kv, cross_out, ff_in, ff_out):
        batch, _, width, channels = latent.shape
        images = batch // num_bands
        tokens = num_bands * latent.shape[1] * width
        groups = res_norm.shape[3]
        heads, head_dim = self_out.shape[:2]
        text = context.shape[1]
        me = lax.axis_index('sp')

        def own(array):
            split = array.reshape((images, num_bands) + array.shape[1:])
            return lax.dynamic_index_in_dim(split, me, 1, keepdims=False)

        own_time, own_context = own(time_emb), own(context)
        norm_cols = res_norm.astype(F32).reshape(2, 4, channels)
        res_cols = []
        for i in range(2):
            shared = jnp.broadcast_to(norm_cols[i][None], (images, 4, channels))
            shared = jnp.concatenate([shared, time_project(own_time, res_time[i])[:, None, :]], axis=1)
            shared = jnp.pad(shared, ((0, 0), (0, groups - 5), (0, 0)))
            res_cols.append(jnp.swapaxes(shared, 1, 2))
        attn_cols = jnp.pad(attn_norm.astype(F32).reshape(2, channels), ((0, groups - 2), (0, 0))).T
        text_pad = -(-text // 16) * 16
        ctx_key = jnp.einsum('btc,chd->bhtd', own_context, cross_kv[0], preferred_element_type=F32).astype(BF16)
        ctx_key = jnp.pad(ctx_key, ((0, 0), (0, 0), (0, text_pad - text), (0, LANES - head_dim)))
        ctx_val = jnp.einsum('btc,chd->bhdt', own_context, cross_kv[1], preferred_element_type=F32).astype(BF16)
        ctx_val = jnp.pad(ctx_val.reshape(images, channels, text), ((0, 0), (0, 0), (0, LANES - text)))
        weights = (proj_inout[0], self_qkv.reshape(3, channels, channels), self_out.reshape(channels, channels), cross_q.reshape(channels, channels), cross_out.reshape(channels, channels), ff_in, ff_out, proj_inout[1])
        conv_weights = res_conv.reshape(4, 9 * channels, channels)

        group_width = channels // groups
        rows, received, later = latent, [], (ctx_key, ctx_val) + weights
        for i in range(images):
            if received:
                rows, later = lax.optimization_barrier((rows, later))
            received.append(lax.all_to_all(rows[i * num_bands:(i + 1) * num_bands], 'sp', 0, 1, tiled=True))
        ctx_key, ctx_val, *weights = later
        before = ()
        for i in range(images):
            before = res_block_in(i, images, received[i].reshape(tokens, channels), res_cols[0], conv_weights, 0, width, group_width, before)
        stacked, parts = former(*before, attn_cols, ctx_key, ctx_val, weights, text, group_width)
        out = res_block_out('sp', num_bands, stacked, parts, res_cols[1], conv_weights, 2, width, group_width)
        return out.reshape(latent.shape)

    band_spec = P('dp', 'sp', None, None)
    shared = P()
    in_specs = (band_spec, P('dp', None), P('dp', None, None)) + (shared,) * 12
    return jax.shard_map(local_stage, mesh=mesh, in_specs=in_specs, out_specs=band_spec, check_vma=False)
```

time: 1330 us -> 337 us (0.25)
  matrix products: 490 us -> 5.94 us
  waiting for transfers between devices: 401 us -> 2.5 us
  Pallas kernels: 0 us -> 288 us
  other arithmetic: 128 us -> 0.78 us
  local copies, waits for them, and re-layouts: 149 us -> 22.7 us
  blocking collectives: 107 us -> 0 us
  starting transfers between devices: 33.6 us -> 11.9 us
  between operations: 14.3 us -> 0.63 us
    dot_general x10 -> x4, matrix products: 333 us -> 5.94 us  [the longest x2 3.51 us: time_project(): return jnp.dot(time_act, weight, preferred_element_type=F32)]
    pallas_call x0 -> x4, Pallas kernels: none -> 288 us  [the longest x1 126 us: former(): pl.pallas_call(functools.partial(former_kernel, heads, text, group_width,...]
    all_gather x2 -> x0, waiting for transfers between devices: 241 us -> none  [the longest x1 165 us: transformer(): lax.all_gather(project(ln_tokens, self_qkv[1]).reshape(band_shape), 'sp',...]
    ppermute x8 -> x0, waiting for transfers between devices: 160 us -> none  [the longest x4 142 us: conv_band(): top_halo = lax.ppermute(act_in[:, -1:], 'sp', to_next)]
    conv_general_dilated x4 -> x0, matrix products: 142 us -> none  [conv_band(): lax.conv_general_dilated(padded, kernel, (1, 1), ((0, 0), (1, 1)), dimens...]
    psum x5 -> x0, blocking collectives: 107 us -> none  [group_norm(): stat_sums = lax.psum(local_sums, 'sp')]
    reshape x8 -> x2, local copies, waits for them, and re-layouts: 90.4 us -> 0.31 us  [local_stage(): attn_norm.astype(F32).reshape(2, channels)]
    reduce_sum x17 -> x0, other arithmetic: 82.8 us -> none  [the longest x2 52.9 us: attend(): row_sum = jnp.sum(weights, axis=-1, keepdims=True)]
  transfers between devices with their start and end apart: 10 -> 2, of which waited for: 10 -> 1; matrix products, arithmetic and copies ran while one was open for 17% -> 6% of each run, Pallas kernels for 0% -> 11%
where the time goes in v1:
time: 337 us; the launch traced here: 332 us
  Pallas kernels  288 us (85%)
  local copies, waits for them, and re-layouts  22.7 us (7%)
  starting transfers between devices  11.9 us (4%)
  matrix products  5.94 us (2%)
    pallas_call x1, Pallas kernels, former(): pl.pallas_call(functools.partial(former_kernel, heads, text, group_width,...  126 us
    pallas_call x1, Pallas kernels, res_block_out(): pl.pallas_call(functools.partial(res_out_kernel, axis, bands, width, grou...  89.4 us
    pallas_call x2, Pallas kernels, res_block_in(): pl.pallas_call(functools.partial(res_in_kernel, width, group_width, first...  72.9 us
    all_to_all x2, starting transfers between devices, local_stage(): lax.all_to_all(rows[i * num_bands:(i + 1) * num_bands], 'sp', 0, 1, tiled...  11.9 us
  transfers between devices with their start and end apart: 2, of which 1 were waited for; matrix products, arithmetic and copies ran while one was open for 6% of the time, Pallas kernels for 11%

profile of v1, /device:TPU:81, one launch (start us, length us, event | category | flops | bytes accessed | tf_op | source)
XLA Modules:
  0.0 332.3 jit_solution(1929523025296199132)
XLA Ops:
  0.0 0.0 copy-start
  0.0 3.1 slice.39
  3.1 6.2 %all-to-all-start.1 = ((bf16[8,1,192,640]{3,2,1,0:T(8,128)(2,1)}), bf16[8,1,192,640]{3,2,1,0:T(8,128)(2,1)}, u32[]{:S(2)}, u32[]{:S(2)}) async-start(bf16[8,1,192,640]{3,2,1,0:T(8,128)(2,1)} %slice.39), calls=%async_computation.1 | async-start | bytes 3932160 | tf_op jit(solution)/shard_map/all_to_all | solution.py:483
  9.4 0.0 copy-done
  9.4 0.5 constant_dynamic-slice_fusion.1
  9.9 1.9 fusion.7
  11.7 0.0 copy-done.8
  11.8 0.0 copy-start.4
  11.8 0.6 fusion.6
  12.3 0.2 copy.39
  12.6 0.8 pad.21.ctx_val_ref
  13.4 0.8 pad.20.ctx_key_ref
  14.2 0.0 copy-done.4
  14.2 1.3 slice_bitcast_fusion
  15.5 0.7 copy-done.3
  16.2 1.4 slice.36
  17.7 0.0 copy-done.6
  17.7 0.1 copy.40
  17.8 0.1 broadcast_in_dim.20
  17.9 0.8 constant_dynamic-slice_fusion
  18.7 1.8 fusion.8
  20.5 0.3 copy.42
  20.8 0.0 copy-start.5
  20.8 0.0 copy-start.7
  20.8 5.2 %copy.45.refs_1_ = bf16[3,640,640]{2,1,0:T(8,128)(2,1)} copy(bf16[3,640,640]{1,2,0:T(8,128)(2,1)} %bitcast.66) | data formatting | bytes 4915200 | tf_op jit(solution)/shard_map/optimization_barrier | solution.py:482
  26.0 0.0 copy-done.5
  26.0 1.3 copy.46.refs_3_
  27.2 0.0 copy-done.7
  27.2 0.1 copy.43
  27.4 0.1 reshape.62
  27.5 0.2 copy.44
  27.7 0.1 copy.47
  27.8 0.1 broadcast_in_dim.23
  27.9 1.8 fusion.11
  29.7 0.3 copy.48
  30.0 0.8 convert_bitcast_fusion.cols_ref
  30.7 0.9 pad_bitcast_fusion.1.cols_ref
  31.7 2.5 all-to-all-done.1
  34.2 5.6 %all-to-all-start = ((bf16[8,1,192,640]{3,2,1,0:T(8,128)(2,1)}), bf16[8,1,192,640]{3,2,1,0:T(8,128)(2,1)}, u32[]{:S(2)}, u32[]{:S(2)}) async-start(bf16[8,1,192,640]{3,2,1,0:T(8,128)(2,1)} %slice.36), calls=%async_computation | async-start | bytes 3932160 | tf_op jit(solution)/shard_map/all_to_all | solution.py:483
  39.8 36.5 %res_in.2 = (bf16[2,640,1536]{2,1,0:T(8,128)(2,1)}, f32[2,640,256]{2,1,0:T(8,128)}) custom-call(bf16[1536,640]{1,0:T(8,128)(2,1)} %bitcast.25.hid_ref, f32[2,640,32]{2,1,0:T(8,128)} %pad_bitcast_fusion.1.cols_ref, bf16[4,5760,640]{2,1,0:T(8,128)(2,1)} %bitcast.70), custom_call_target="tpu_custom_call" | custom-call | flops 22649241600 | bytes 16384000 | tf_op jit(solution)/shard_map/res_in/pallas_call | solution.py:237
  76.3 0.0 all-to-all-done
  76.3 36.4 %res_in.3 = (bf16[2,640,1536]{2,1,0:T(8,128)(2,1)}, f32[2,640,256]{2,1,0:T(8,128)}) custom-call(bf16[1536,640]{1,0:T(8,128)(2,1)} %bitcast.18.hid_ref, f32[2,640,32]{2,1,0:T(8,128)} %pad_bitcast_fusion.1.cols_ref, bf16[4,5760,640]{2,1,0:T(8,128)(2,1)} %bitcast.71, ...), custom_call_target="tpu_custom_call", output_to_operand_aliasing={{0}: (3, {}), {1}: (4, {})} | custom-call | flops 22649241600 | bytes 16384000 | tf_op jit(solution)/shard_map/res_in/pallas_call | solution.py:237
  112.7 125.6 %former.1 = (bf16[2,640,1536]{2,1,0:T(8,128)(2,1)}, f32[2,640,256]{2,1,0:T(8,128)}) custom-call(bf16[2,640,1536]{2,1,0:T(8,128)(2,1)} %get-tuple-element.25.hid_ref, f32[2,640,256]{2,1,0:T(8,128)} %get-tuple-element.26.part_in_ref, f32[640,32]{1,0:T(8,128)} %convert_bitcast_fusion.cols_ref, bf16[2,8,80,128]{3,2,1,0:T(8,128)(2,1)} %pad.20.ctx_key_ref, ...), custom_call_target="tpu_custom_call" | custom-call | flops 86570434560 | bytes 62914560 | tf_op jit(solution)/shard_map/former/pallas_call | solution.py:422
  238.4 1.3 copy-done.2
  239.7 89.4 %res_out.1 = bf16[16,192,640]{2,1,0:T(8,128)(2,1)S(1)} custom-call(bf16[2,640,1536]{2,1,0:T(8,128)(2,1)} %get-tuple-element.37.hid_ref, f32[2,640,256]{2,1,0:T(8,128)S(1)} %copy-done.2, f32[2,640,32]{2,1,0:T(8,128)S(1)} %pad_bitcast_fusion.cols_ref, bf16[4,5760,640]{2,1,0:T(8,128)(2,1)} %bitcast.72), custom_call_target="tpu_custom_call" | custom-call | flops 45298483200 | bytes 16384000 | tf_op jit(solution)/shard_map/res_out/pallas_call | solution.py:257
  329.0 0.0 copy-start.1
  329.0 2.0 copy.62
  331.0 0.9 copy-done.1
  (10 shorter events, 0.1 us)
Async XLA Ops:
  0.0 9.4 %copy-start = (bf16[16,77,768]{2,0,1:T(8,128)(2,1)S(1)}, bf16[16,77,768]{2,0,1:T(8,128)(2,1)}, u32[]{:S(2)}) copy-start(bf16[16,77,768]{2,0,1:T(8,128)(2,1)} %param.17) | copy-start | bytes 5677060
  3.1 31.0 %all-to-all-start.1 = ((bf16[8,1,192,640]{3,2,1,0:T(8,128)(2,1)}), bf16[8,1,192,640]{3,2,1,0:T(8,128)(2,1)}, u32[]{:S(2)}, u32[]{:S(2)}) async-start(bf16[8,1,192,640]{3,2,1,0:T(8,128)(2,1)} %slice.39), calls=%async_computation.1 | async-start | bytes 3932160 | tf_op jit(solution)/shard_map/all_to_all | solution.py:483
  9.4 2.4 copy-start.8
  11.8 2.5 copy-start.4
  13.4 2.8 copy-start.3
  16.2 1.4 copy-start.6
  20.8 5.2 %copy-start.5 = (bf16[640,8,80]{0,2,1:T(8,128)(2,1)S(1)}, bf16[640,8,80]{0,2,1:T(8,128)(2,1)}, u32[]{:S(2)}) copy-start(bf16[640,8,80]{0,2,1:T(8,128)(2,1)} %param.25) | copy-start | bytes 2457604
  20.8 6.5 %copy-start.7 = (bf16[2,32,20]{1,0,2:T(2,128)(2,1)S(1)}, bf16[2,32,20]{1,0,2:T(2,128)(2,1)}, u32[]{:S(2)}) copy-start(bf16[2,32,20]{1,0,2:T(2,128)(2,1)} %param.21) | copy-start | bytes 7684
  34.2 42.1 %all-to-all-start = ((bf16[8,1,192,640]{3,2,1,0:T(8,128)(2,1)}), bf16[8,1,192,640]{3,2,1,0:T(8,128)(2,1)}, u32[]{:S(2)}, u32[]{:S(2)}) async-start(bf16[8,1,192,640]{3,2,1,0:T(8,128)(2,1)} %slice.36), calls=%async_computation | async-start | bytes 3932160 | tf_op jit(solution)/shard_map/all_to_all | solution.py:483
  238.4 1.3 copy-start.2
  329.0 2.9 copy-start.1

commit v2 on v1

v2 whole, which is shorter than its diff:
```python
import functools
import math
import jax
import jax.numpy as jnp
from jax import lax
from jax.experimental import pallas as pl
from jax.experimental.pallas import tpu as pltpu
from jax.sharding import PartitionSpec as P

GN_EPS = 1e-6
LN_EPS = 1e-5
LANES = 128
SUBLANES = 8
MESH = pl.DeviceIdType.MESH
LOGIT_LIMIT = 60.0
VALUE_LIMIT = 1e8
MIB = 2 ** 20
F32 = jnp.float32
BF16 = jnp.bfloat16
LHS_T = (((0,), (0,)), ((), ()))
BOTH_T = (((0,), (1,)), ((), ()))
LAST = (((1,), (1,)), ((), ()))


def tdot(weight, act):
    return lax.dot_general(weight, act, LHS_T, preferred_element_type=F32)


def lane_sum(parts, value):
    total = parts
    for off in range(0, value.shape[1], LANES):
        total = total + value[:, off:off + LANES]
    return total


def group_affine(sums, squares, width, count, gain, shift):
    span = math.lcm(width, SUBLANES)
    row = lax.broadcasted_iota(jnp.int32, (SUBLANES, LANES), 0)
    scales, offsets = [], []

    def group_mean(array, base, low, high):
        total = None
        for top in range(0, span, SUBLANES):
            first, last = max(low - top, 0), min(high - top, SUBLANES)
            if first < last:
                tile = array[base + top:base + top + SUBLANES]
                if last - first < SUBLANES:
                    tile = jnp.where((row >= first) & (row < last), tile, 0.0)
                total = tile if total is None else total + tile
        for turn in (4, 2, 1):
            total = total + pltpu.roll(total, turn, 0)
        return jnp.broadcast_to(jnp.sum(total, axis=1, keepdims=True), (SUBLANES, LANES)) / count

    for base in range(0, sums.shape[0], span):
        means, rstds = [], []
        for low in range(0, span, width):
            mean = group_mean(sums, base, low, low + width)
            means.append(mean)
            rstds.append(lax.rsqrt(group_mean(squares, base, low, low + width) - mean * mean + GN_EPS))
        for top in range(0, span, SUBLANES):
            mean, rstd = means[top // width], rstds[top // width]
            for nxt in range(top // width + 1, (top + SUBLANES - 1) // width + 1):
                mean = jnp.where(row >= nxt * width - top, means[nxt], mean)
                rstd = jnp.where(row >= nxt * width - top, rstds[nxt], rstd)
            here = slice(base + top, base + top + SUBLANES)
            scale = rstd * gain[here]
            scales.append(scale)
            offsets.append(shift[here] - mean * scale)
    return jnp.concatenate(scales, axis=0), jnp.concatenate(offsets, axis=0)


def affine(block, scale, offset):
    pieces = [block[:, off:off + LANES].astype(F32) * scale + offset for off in range(0, block.shape[1], LANES)]
    return jnp.concatenate(pieces, axis=1)


def layer_norm(tokens):
    centred = tokens - jnp.mean(tokens, axis=0, keepdims=True)
    return (centred * lax.rsqrt(jnp.mean(centred * centred, axis=0, keepdims=True) + LN_EPS)).astype(BF16)


def res_phase(which, first, width, group_width, hid, cols, cur, wide, aff, weight, sums, squares, conv_block, order, keep, emit):
    channels, tokens = cur.shape
    count = float(tokens * group_width)
    gain = jnp.where(first, cols[:, 0:1], cols[:, 2:3])
    shift = jnp.where(first, cols[:, 1:2], cols[:, 3:4])
    scale, offset = group_affine(sums, squares, group_width, count, gain, shift)
    aff[0], aff[1] = 0.5 * scale, 0.5 * offset
    act_block, edge = 2 * width, 16
    row = lax.broadcasted_iota(jnp.int32, (edge, channels), 0)

    def widen(i, carry):
        tok = pl.ds(pl.multiple_of(i * act_block, LANES), act_block)
        half = affine(cur[:, tok], aff[0], aff[1])
        act = (half + half * jnp.tanh(half)).T
        left, right = pltpu.roll(act, 1, 0), pltpu.roll(act, act_block - 1, 0)

        def put(tap, base, value):
            dst = pl.ds(pl.multiple_of(i * act_block + width + base, edge), value.shape[0])
            wide[dst, tap * channels:(tap + 1) * channels] = value.astype(BF16)

        put(1, 0, act)
        for base in range(0, act_block, width):
            put(0, base, jnp.where(row == 0, 0.0, left[base:base + edge]))
            put(0, base + edge, left[base + edge:base + width])
            put(2, base, right[base:base + width - edge])
            put(2, base + width - edge, jnp.where(row == edge - 1, 0.0, right[base + width - edge:base + width]))
        return carry

    lax.fori_loop(0, tokens // act_block, widen, 0)
    if weight[1] is not None:
        weight[1].wait()
    time_term = cols[:, 4:5]
    cut = -(-channels // LANES // 2) * LANES

    def convolve(i, carry):
        block = order(i)
        start = block * conv_block
        tok = pl.ds(pl.multiple_of(start, LANES), conv_block)
        taps_in = jnp.concatenate([wide[pl.ds(pl.multiple_of(start + dy * width, 64), conv_block), :] for dy in range(3)], axis=1)
        sums, squares = [], []
        for low, high in ((0, cut), (cut, channels)):
            value = lax.dot_general(weight[0][which, :, low:high], taps_in, BOTH_T, preferred_element_type=F32)
            out = value + jnp.where(first, time_term[low:high], hid[low:high, tok].astype(F32))
            cur[low:high, tok] = out.astype(BF16)
            keep(tok, low, high, out)
            out = out.astype(BF16).astype(F32)
            sums.append(lane_sum(carry[0][low:high], out))
            squares.append(lane_sum(carry[1][low:high], out * out))
        emit(block)
        return jnp.concatenate(sums, axis=0), jnp.concatenate(squares, axis=0)

    zero = jnp.zeros((channels, LANES), F32)
    return lax.fori_loop(0, tokens // conv_block, convolve, (zero, zero))


def clear_border(wide, width):
    rows, taps = wide.shape
    wide[0:width, :] = jnp.zeros((width, taps), BF16)
    wide[rows - width:rows, :] = jnp.zeros((width, taps), BF16)


def weight_copies(weight_hbm, weight_scr, sems, first_conv):
    return lambda i: pltpu.make_async_copy(weight_hbm.at[first_conv + i], weight_scr.at[i], sems.at[i])


def greet(axis, bands, me):
    barrier = pltpu.get_barrier_semaphore()
    for step in range(1, bands):
        pl.semaphore_signal(barrier, inc=1, device_id={axis: lax.rem(me + step, bands)}, device_id_type=MESH)
    return lambda: pl.semaphore_wait(barrier, bands - 1)


def entry_kernel(axis, bands, latent_hbm, time_ref, ctx_ref, norm_ref, time_w_hbm, ctx_w_hbm, first_hbm, cols_one_ref, cols_two_ref, key_ref, val_ref, time_scr, ctx_scr, send_sems, recv_sems, own_sems):
    me = lax.axis_index(axis)
    everyone_here = greet(axis, bands, me)

    def remote(peer, source):
        return pltpu.make_async_remote_copy(
            src_ref=latent_hbm.at[peer, 0], dst_ref=first_hbm.at[source],
            send_sem=send_sems.at[peer], recv_sem=recv_sems.at[source], device_id={axis: peer}, device_id_type=MESH)

    own = pltpu.make_async_copy(latent_hbm.at[me, 0], first_hbm.at[me], own_sems.at[0])
    everyone_here()
    for step in range(1, bands):
        remote(lax.rem(me + step, bands), me).start()
    loads = [pltpu.make_async_copy(time_w_hbm, time_scr, own_sems.at[1]), pltpu.make_async_copy(ctx_w_hbm, ctx_scr, own_sems.at[2])]
    own.start()
    for load in loads:
        load.start()
    images, heads, text_pad, _ = key_ref.shape
    channels = val_ref.shape[1]
    head_dim = channels // heads
    half = 0.5 * time_ref[...].astype(F32)
    time_act = (half + half * jnp.tanh(half)).astype(BF16)
    lane = lax.broadcasted_iota(jnp.int32, norm_ref.shape[1:], 1)
    loads[0].wait()
    for block, cols_ref in enumerate((cols_one_ref, cols_two_ref)):
        term = lax.dot_general(time_scr[block], time_act, BOTH_T, preferred_element_type=F32)
        place = lax.broadcasted_iota(jnp.int32, term.shape, 1)
        for j in range(images):
            mine = jnp.sum(jnp.where(place == j * bands + me, term, 0.0), axis=1, keepdims=True)
            cols_ref[j] = jnp.where(lane == 4, mine, norm_ref[block])
    loads[1].wait()
    pad = jnp.zeros((LANES - head_dim, LANES), BF16)
    for j in range(images):
        key = lax.dot_general(ctx_scr[0], ctx_ref[j], LAST, preferred_element_type=F32).astype(BF16)
        for h in range(heads):
            key_ref[j, h] = jnp.concatenate([key[h * head_dim:(h + 1) * head_dim], pad], axis=0).T[0:text_pad]
        val_ref[j] = lax.dot_general(ctx_scr[1], ctx_ref[j], LAST, preferred_element_type=F32).astype(BF16)
    for step in range(1, bands):
        peer = lax.rem(me + step, bands)
        remote(peer, me).wait_send()
        remote(peer, peer).wait_recv()
    own.wait()


def entry(axis, bands, images, heads, text_pad, latent, time_emb, own_context, norm_cols, time_w, ctx_w):
    _, _, width, channels = latent.shape
    vmem, hbm = pl.BlockSpec(memory_space=pltpu.VMEM), pl.BlockSpec(memory_space=pltpu.HBM)
    cols = jax.ShapeDtypeStruct((images,) + norm_cols.shape[1:], F32)
    return pl.pallas_call(
        functools.partial(entry_kernel, axis, bands),
        out_shape=(jax.ShapeDtypeStruct((bands, width, channels), BF16), cols, cols, jax.ShapeDtypeStruct((images, heads, text_pad, LANES), BF16), jax.ShapeDtypeStruct((images, channels, LANES), BF16)),
        in_specs=[hbm, vmem, vmem, vmem, hbm, hbm],
        out_specs=(hbm, vmem, vmem, vmem, vmem),
        scratch_shapes=[pltpu.VMEM(time_w.shape, BF16), pltpu.VMEM(ctx_w.shape, BF16), pltpu.SemaphoreType.DMA((bands,)), pltpu.SemaphoreType.DMA((bands,)), pltpu.SemaphoreType.DMA((3,))],
        name='entry',
        cost_estimate=pl.CostEstimate(flops=10 ** 9, bytes_accessed=8 * MIB, transcendentals=0),
        compiler_params=pltpu.CompilerParams(vmem_limit_bytes=60 * MIB, collective_id=8, has_side_effects=True),
    )(latent, time_emb, own_context, norm_cols, time_w, ctx_w)


def res_in_kernel(axis, bands, image, sending, width, group_width, first_conv, conv_block, hid_ref, cols_ref, weight_hbm, *refs):
    if sending:
        latent_hbm, (next_hbm, *refs), sync = refs[0], refs[-11:-3], refs[-3:]
        send_sems, recv_sems, own_sem = sync
        out_ref, parts_ref = refs[:2]
    out_ref, parts_ref, hid_scr, wide_scr, aff_scr, weight_scr, sems = refs[-7:]
    channels, tokens = hid_scr.shape
    copies = weight_copies(weight_hbm, weight_scr, sems, first_conv)
    for i in range(2):
        copies(i).start()
    if sending:
        me = lax.axis_index(axis)
        everyone_here = greet(axis, bands, me)
    clear_border(wide_scr, width)
    act_block = 2 * width
    cur = out_ref.at[0]

    def load(i, carry):
        tok = pl.ds(pl.multiple_of(i * act_block, LANES), act_block)
        block = hid_ref[tok, :].astype(F32).T
        hid_scr[:, tok] = block.astype(BF16)
        cur[:, tok] = block.astype(BF16)
        return lane_sum(carry[0], block), lane_sum(carry[1], block * block)

    zero = jnp.zeros((channels, LANES), F32)
    stats = lax.fori_loop(0, tokens // act_block, load, (zero, zero))

    if sending:
        def remote(peer, source):
            return pltpu.make_async_remote_copy(
                src_ref=latent_hbm.at[(image + 1) * bands + peer, 0], dst_ref=next_hbm.at[source],
                send_sem=send_sems.at[peer], recv_sem=recv_sems.at[source], device_id={axis: peer}, device_id_type=MESH)

        own = pltpu.make_async_copy(latent_hbm.at[(image + 1) * bands + me, 0], next_hbm.at[me], own_sem.at[0])
        everyone_here()
        for step in range(1, bands):
            remote(lax.rem(me + step, bands), me).start()
        own.start()

    def half(which, stats):
        return res_phase(which, which == 0, width, group_width, hid_scr, cols_ref[0], cur, wide_scr, aff_scr, (weight_scr, copies(which)), *stats, conv_block, lambda i: i, lambda *piece: None, lambda block: None)

    sums, squares = lax.fori_loop(0, 2, half, stats)
    parts_ref[0, :, 0:LANES] = sums
    parts_ref[0, :, LANES:2 * LANES] = squares
    if sending:
        for step in range(1, bands):
            peer = lax.rem(me + step, bands)
            remote(peer, me).wait_send()
            remote(peer, peer).wait_recv()
        own.wait()


def res_out_kernel(axis, bands, width, group_width, first_conv, conv_block, hid_hbm, parts_ref, cols_ref, weight_hbm, out_hbm, hid_ref, cur_scr, wide_scr, aff_scr, rows_scr, weight_scr, hid_sems, sems, send_sems, recv_sems, own_sems):
    images, channels, tokens = hid_ref.shape
    fetches = [pltpu.make_async_copy(hid_hbm.at[i], hid_ref.at[i], hid_sems.at[i]) for i in range(images)]
    for fetch in fetches:
        fetch.start()
    band = tokens // bands
    me = lax.axis_index(axis)
    copies = weight_copies(weight_hbm, weight_scr, sems, first_conv)
    for i in range(2):
        copies(i).start()
    everyone_here = greet(axis, bands, me)
    clear_border(wide_scr, width)
    everyone_here()
    for fetch in fetches:
        fetch.wait()

    blocks = tokens // conv_block
    stride = jnp.where(lax.rem(me, 2) == 0, 1, blocks - 1)

    def order(i):
        return lax.rem(lax.div(me * band, conv_block) + (i + 1) * stride, blocks)

    def remote(image, peer, source, low=0, high=band, to=None):
        to = peer if to is None else to
        return pltpu.make_async_remote_copy(
            src_ref=rows_scr.at[image, pl.ds(peer * band + low, high - low)], dst_ref=out_hbm.at[image * bands + source, pl.ds(low, high - low)],
            send_sem=send_sems.at[image, to], recv_sem=recv_sems.at[image, source], device_id={axis: to}, device_id_type=MESH)

    def local(image, peer, low=0, high=band):
        return pltpu.make_async_copy(rows_scr.at[image, pl.ds(peer * band + low, high - low)], out_hbm.at[image * bands + me, pl.ds(low, high - low)], own_sems.at[image])

    def per_image(image, carry):
        cur_scr[...] = hid_ref[image]

        def half(which, stats):
            def keep(tok, low, high, out):
                rows_scr[image, tok, low:high] = out.T.astype(BF16)

            def emit(block):
                for ready in range(tokens // conv_block):
                    for peer in range(bands):
                        low = max(ready * conv_block - peer * band, 0)
                        high = min((ready + 1) * conv_block - peer * band, band)
                        if low >= high:
                            continue
                        now = (which == 1) & (block == ready)

                        @pl.when(now & (me != peer))
                        def _():
                            remote(image, peer, me, low, high).start()

                        @pl.when(now & (me == peer))
                        def _():
                            local(image, peer, low, high).start()

            @pl.when((image == 0))
            def _():
                copies(which).wait()

            return res_phase(which, which == 0, width, group_width, hid_ref.at[image], cols_ref[image], cur_scr, wide_scr, aff_scr, (weight_scr, None), *stats, conv_block, order, keep, emit)

        lax.fori_loop(0, 2, half, (parts_ref[image, :, 0:LANES], parts_ref[image, :, LANES:2 * LANES]))
        return carry

    lax.fori_loop(0, images, per_image, 0)
    def settle(i, carry):
        image, peer = lax.div(i, bands - 1), lax.rem(me + 1 + lax.rem(i, bands - 1), bands)
        remote(image, 0, peer, to=peer).wait_recv()
        remote(image, 0, me, to=peer).wait_send()
        return carry

    lax.fori_loop(0, images * (bands - 1), settle, 0)
    for image in range(images):
        local(image, 0).wait()


def res_cost(images, channels, tokens):
    return pl.CostEstimate(flops=2 * 2 * 9 * images * channels * channels * tokens, bytes_accessed=40 * channels * channels, transcendentals=0)


def res_block_in(axis, bands, image, images, hid, latent, cols, weights, first_conv, width, group_width, before):
    tokens, channels = hid.shape
    conv_block, taps = 512, 3 * channels
    sending = image + 1 < images
    slot = lambda i: (image, 0, 0)
    any_spec, hbm = pl.BlockSpec(memory_space=pl.ANY), pl.BlockSpec(memory_space=pltpu.HBM)
    extra = (latent,) if sending else ()
    start = 3 + len(extra)
    received = (jax.ShapeDtypeStruct((bands, tokens // bands, channels), BF16),) if sending else ()
    params = dict(collective_id=1 + image, has_side_effects=True) if sending else {}
    result = pl.pallas_call(
        functools.partial(res_in_kernel, axis, bands, image, sending, width, group_width, first_conv, conv_block),
        grid=(1,),
        out_shape=received + (jax.ShapeDtypeStruct((images, channels, tokens), BF16), jax.ShapeDtypeStruct((images, channels, 2 * LANES), F32)),
        in_specs=[pl.BlockSpec(hid.shape, lambda i: (0, 0)), pl.BlockSpec((1,) + cols.shape[1:], slot), hbm] + [hbm] * len(extra) + [any_spec] * len(before),
        out_specs=(hbm,) * len(received) + (pl.BlockSpec((1, channels, tokens), slot), pl.BlockSpec((1, channels, 2 * LANES), slot)),
        scratch_shapes=[
            pltpu.VMEM((channels, tokens), BF16), pltpu.VMEM((tokens + 2 * width, taps), BF16),
            pltpu.VMEM((2, channels, LANES), F32), pltpu.VMEM((2, 3 * taps, channels), BF16), pltpu.SemaphoreType.DMA((2,))]
        + [pltpu.SemaphoreType.DMA((bands,)), pltpu.SemaphoreType.DMA((bands,)), pltpu.SemaphoreType.DMA((1,))] * sending,
        input_output_aliases={start + i: len(received) + i for i in range(len(before))},
        name='res_in',
        cost_estimate=res_cost(1, channels, tokens),
        compiler_params=pltpu.CompilerParams(vmem_limit_bytes=62 * MIB, **params),
    )(hid, cols, weights, *extra, *before)
    return (result[0] if sending else None), result[-2:]


def res_block_out(axis, bands, stacked, parts, cols, weights, first_conv, width, group_width):
    images, channels, tokens = stacked.shape
    conv_block, taps = 512, 3 * channels
    vmem = pl.BlockSpec(memory_space=pltpu.VMEM)
    return pl.pallas_call(
        functools.partial(res_out_kernel, axis, bands, width, group_width, first_conv, conv_block),
        out_shape=jax.ShapeDtypeStruct((images * bands, tokens // bands, channels), BF16),
        in_specs=[pl.BlockSpec(memory_space=pltpu.HBM), vmem, vmem, pl.BlockSpec(memory_space=pltpu.HBM)],
        out_specs=pl.BlockSpec(memory_space=pltpu.HBM),
        scratch_shapes=[
            pltpu.VMEM(stacked.shape, BF16), pltpu.VMEM((channels, tokens), BF16), pltpu.VMEM((tokens + 2 * width, taps), BF16),
            pltpu.VMEM((2, channels, LANES), F32), pltpu.VMEM((images, tokens, channels), BF16), pltpu.VMEM((2, 3 * taps, channels), BF16),
            pltpu.SemaphoreType.DMA((images,)), pltpu.SemaphoreType.DMA((2,)), pltpu.SemaphoreType.DMA((images, bands)), pltpu.SemaphoreType.DMA((images, bands)), pltpu.SemaphoreType.DMA((images,))],
        name='res_out',
        cost_estimate=res_cost(images, channels, tokens),
        compiler_params=pltpu.CompilerParams(vmem_limit_bytes=48 * MIB, collective_id=0, has_side_effects=True),
    )(stacked, parts, cols, weights)


def former_kernel(heads, text, group_width, block, q_block, k_chunk, hid_ref, part_in_ref, cols_ref, ctx_key_ref, ctx_val_ref, *refs):
    weights_hbm, refs = refs[:7], refs[7:]
    out_ref, parts_ref, tok_scr, query_scr, key_scr, val_scr, att_scr, logit_scr, prob_scr, cross_scr, gate_scr, two_scr, normed_scr = refs[:13]
    weights, sems = refs[13:20], refs[20]
    _, channels, tokens = hid_ref.shape
    head_dim = channels // heads
    ff_width = weights[6].shape[0]
    count = float(tokens * group_width)
    exp_scale = head_dim ** -0.5 * 1.4426950408889634
    first = pl.program_id(0) == 0
    copies = [pltpu.make_async_copy(weights_hbm[i], weights[i], sems.at[i]) for i in range(7)]

    @pl.when(first)
    def _():
        for copy in copies:
            copy.start()
        query_scr[...] = jnp.zeros(query_scr.shape, BF16)

    def ready(*which):
        @pl.when(first)
        def _():
            for i in which:
                copies[i].wait()

    scale, offset = group_affine(part_in_ref[0, :, 0:LANES], part_in_ref[0, :, LANES:2 * LANES], group_width, count, cols_ref[:, 0:1], cols_ref[:, 1:2])
    ready(0, 1)
    pad = jnp.zeros((query_scr.shape[1] - head_dim, block), BF16)

    split = block // 2

    def largest(value, before):
        square = value.astype(F32)
        square = (square * square).reshape(heads, head_dim, value.shape[1])
        return jnp.maximum(jnp.sum(square, axis=1), before)

    def project(i, carry):
        toks = [pl.ds(pl.multiple_of(i * block + off, LANES), split) for off in range(0, block, split)]
        tokens_in = [tdot(weights[0][0], affine(hid_ref[0, :, tok], scale, offset).astype(BF16)).astype(BF16) for tok in toks]
        normed = [layer_norm(token.astype(F32)) for token in tokens_in]
        for tok, token in zip(toks, tokens_in):
            tok_scr[:, tok] = token
        for tok, norm in zip(toks, normed):
            query = jnp.dot(weights[1][0], norm, preferred_element_type=F32).astype(BF16)
            key = jnp.dot(weights[1][1], norm, preferred_element_type=F32).astype(BF16)
            value = jnp.dot(weights[1][2], norm, preferred_element_type=F32).astype(BF16)
            val_scr[:, tok] = value
            for h in range(heads):
                query_scr[h, 0:head_dim, tok] = query[h * head_dim:(h + 1) * head_dim]
                key_scr[h, tok, :] = jnp.concatenate([key[h * head_dim:(h + 1) * head_dim], pad[:, 0:split]], axis=0).T
            carry = largest(query, carry[0]), largest(key, carry[1]), largest(value, carry[2])
        return carry

    zero = jnp.zeros((heads, split), F32)
    norms = lax.fori_loop(0, tokens // block, project, (zero, zero, zero))
    query_norm, key_norm, value_norm = [jnp.max(norm, axis=1, keepdims=True) for norm in norms]
    logit_bound = jnp.max(query_norm * key_norm) / head_dim
    small = (logit_bound <= LOGIT_LIMIT ** 2) & (jnp.max(value_norm) <= VALUE_LIMIT ** 2)
    blocks, chunks = tokens // q_block, tokens // k_chunk

    def fold(combine, part):
        return combine(part.reshape(k_chunk // SUBLANES, SUBLANES, q_block), axis=0)

    def logits(h, cols, c):
        return jnp.dot(key_scr[h, c * k_chunk:(c + 1) * k_chunk, :], query_scr[h, :, cols], preferred_element_type=F32)

    def weigh(h, cols, slot, total):
        head = pl.ds(pl.multiple_of(h * head_dim, 16), head_dim)
        mixed = jnp.dot(val_scr[head, :], prob_scr[slot], preferred_element_type=F32)
        att_scr[head, cols] = (mixed * (1.0 / total)).astype(BF16)

    def attend(h, last_total):
        for b in range(blocks):
            cols = slice(b * q_block, (b + 1) * q_block)
            total = 0.0
            for c in range(chunks):
                prob = jnp.exp2(logits(h, cols, c) * exp_scale)
                total = total + fold(jnp.sum, prob)
                prob_scr[b % 2, c * k_chunk:(c + 1) * k_chunk, :] = prob.astype(BF16)
                if c == 1:
                    done = (b - 1) % blocks
                    weigh(h if b else jnp.maximum(h - 1, 0), slice(done * q_block, (done + 1) * q_block), done % 2, last_total)
            last_total = jnp.sum(total, axis=0, keepdims=True)
        return last_total

    @pl.when(small)
    def _():
        prob_scr[(blocks - 1) % 2] = jnp.zeros(prob_scr.shape[1:], BF16)
        total = lax.fori_loop(0, heads, attend, jnp.ones((1, q_block), F32))
        weigh(heads - 1, slice((blocks - 1) * q_block, blocks * q_block), (blocks - 1) % 2, total)

    @pl.when(jnp.logical_not(small))
    def _():
        def attend_shifted(i, carry):
            h = lax.div(i, blocks)
            cols = pl.ds(pl.multiple_of(lax.rem(i, blocks) * q_block, LANES), q_block)
            peak = None
            for c in range(chunks):
                part = logits(h, cols, c)
                logit_scr[c * k_chunk:(c + 1) * k_chunk, :] = part
                peak = fold(jnp.max, part) if peak is None else jnp.maximum(peak, fold(jnp.max, part))
            peak = jnp.max(peak, axis=0, keepdims=True)
            total = 0.0
            for c in range(chunks):
                prob = jnp.exp2((logit_scr[c * k_chunk:(c + 1) * k_chunk, :] - peak) * exp_scale)
                total = total + fold(jnp.sum, prob)
                prob_scr[0, c * k_chunk:(c + 1) * k_chunk, :] = prob.astype(BF16)
            weigh(h, cols, 0, jnp.sum(total, axis=0, keepdims=True))
            return carry

        lax.fori_loop(0, heads * blocks, attend_shifted, 0)

    ready(2, 3, 4, 5, 6)
    text_pad = ctx_key_ref.shape[2]
    text_row = lax.broadcasted_iota(jnp.int32, (text_pad, block), 0)
    cross_pad = jnp.zeros((LANES - text_pad, block), BF16)

    def finish(i, carry):
        start = pl.multiple_of(i * block, LANES)
        tok = pl.ds(start, block)
        split = block // 2
        halves = [slice(off, off + split) for off in range(0, block, split)]
        toks = [pl.ds(pl.multiple_of(start + half.start, LANES), split) for half in halves]
        ones = [(tok_scr[:, t].astype(F32) + tdot(weights[2][...], att_scr[:, t])).astype(BF16) for t in toks]
        queries = [jnp.dot(weights[3][...], layer_norm(one.astype(F32)), preferred_element_type=F32).astype(BF16) for one in ones]
        for h in range(heads):
            head = slice(h * head_dim, (h + 1) * head_dim)
            for half, query in zip(halves, queries):
                logit = jnp.dot(ctx_key_ref[0, h], jnp.concatenate([query[head], pad[:, half]], axis=0), preferred_element_type=F32)
                logit = jnp.where(text_row[:, half] < text, logit, -jnp.inf)
                prob = jnp.exp2((logit - jnp.max(logit, axis=0, keepdims=True)) * exp_scale)
                total = jnp.sum(prob, axis=0, keepdims=True)
                mixed = jnp.dot(ctx_val_ref[0, head, :], jnp.concatenate([prob.astype(BF16), cross_pad[:, half]], axis=0), preferred_element_type=F32)
                cross_scr[head, half] = (mixed * (1.0 / total)).astype(BF16)
        for half, one in zip(halves, ones):
            two = (one.astype(F32) + tdot(weights[4][...], cross_scr[:, half])).astype(BF16)
            two_scr[:, half] = two
            normed_scr[:, half] = layer_norm(two.astype(F32))
        normed = normed_scr[...]
        chunk = channels
        for off in range(0, ff_width, chunk):
            value = tdot(weights[5][:, off:off + chunk], normed)
            gate = tdot(weights[5][:, ff_width + off:ff_width + off + chunk], normed)
            gate_scr[off:off + chunk, :] = (value * (0.5 * gate * (1.0 + lax.erf(gate * (0.5 ** 0.5))))).astype(BF16)
        tok_three = (two_scr[...].astype(F32) + tdot(weights[6][...], gate_scr[...])).astype(BF16)
        out = (hid_ref[0, :, tok].astype(F32) + tdot(weights[0][1], tok_three)).astype(BF16)
        out_ref[0, :, tok] = out
        out = out.astype(F32)
        return lane_sum(carry[0], out), lane_sum(carry[1], out * out)

    zero = jnp.zeros((channels, LANES), F32)
    sums, squares = lax.fori_loop(0, tokens // block, finish, (zero, zero))
    parts_ref[0, :, 0:LANES] = sums
    parts_ref[0, :, LANES:2 * LANES] = squares


def former(stacked, parts, cols, ctx_key, ctx_val, weights, text, group_width):
    images, channels, tokens = stacked.shape
    heads = ctx_key.shape[1]
    block, q_block, k_chunk = 512, 256, 256
    per_image = lambda a: pl.BlockSpec((1,) + a.shape[1:], lambda i: (i,) + (0,) * (a.ndim - 1))
    whole = lambda a: pl.BlockSpec(a.shape, lambda i: (0,) * a.ndim)
    ff_width = weights[6].shape[0]
    flops = 2 * images * tokens * (channels * channels * 8 + 3 * channels * ff_width + 2 * tokens * channels * 3)
    return pl.pallas_call(
        functools.partial(former_kernel, heads, text, group_width, block, q_block, k_chunk),
        grid=(images,),
        out_shape=(jax.ShapeDtypeStruct(stacked.shape, BF16), jax.ShapeDtypeStruct(parts.shape, F32)),
        in_specs=[per_image(stacked), per_image(parts), whole(cols), per_image(ctx_key), per_image(ctx_val)] + [pl.BlockSpec(memory_space=pltpu.HBM)] * len(weights),
        out_specs=(per_image(stacked), per_image(parts)),
        scratch_shapes=[
            pltpu.VMEM((channels, tokens), BF16), pltpu.VMEM((heads, LANES, tokens), BF16), pltpu.VMEM((heads, tokens, LANES), BF16),
            pltpu.VMEM((channels, tokens), BF16), pltpu.VMEM((channels, tokens), BF16),
            pltpu.VMEM((tokens, q_block), F32), pltpu.VMEM((2, tokens, q_block), BF16),
            pltpu.VMEM((channels, block), BF16), pltpu.VMEM((ff_width, block), BF16), pltpu.VMEM((channels, block), BF16), pltpu.VMEM((channels, block), BF16)]
        + [pltpu.VMEM(w.shape, BF16) for w in weights] + [pltpu.SemaphoreType.DMA((len(weights),))],
        name='former',
        cost_estimate=pl.CostEstimate(flops=flops, bytes_accessed=60 * MIB, transcendentals=0),
        compiler_params=pltpu.CompilerParams(vmem_limit_bytes=60 * MIB),
    )(stacked, parts, cols, ctx_key, ctx_val, *weights)


def solution(mesh):
    num_bands = mesh.shape['sp']

    def local_stage(latent, time_emb, context, res_conv, res_time, res_norm, attn_norm, proj_inout, self_qkv, self_out, cross_q, cross_kv, cross_out, ff_in, ff_out):
        batch, _, width, channels = latent.shape
        images = batch // num_bands
        tokens = num_bands * latent.shape[1] * width
        groups = res_norm.shape[3]
        heads, head_dim = self_out.shape[:2]
        text = context.shape[1]
        me = lax.axis_index('sp')

        def own(array):
            split = array.reshape((images, num_bands) + array.shape[1:])
            return lax.dynamic_index_in_dim(split, me, 1, keepdims=False)

        group_width = channels // groups
        text_pad = -(-text // 16) * 16
        own_context = jnp.pad(own(context), ((0, 0), (0, LANES - text), (0, 0)))
        norm_cols = jnp.swapaxes(jnp.pad(res_norm.astype(F32).reshape(2, 4, channels), ((0, 0), (0, 4), (0, 0))), 1, 2)
        attn_cols = jnp.pad(attn_norm.astype(F32).reshape(2, channels), ((0, 6), (0, 0))).T
        ctx_w = jnp.transpose(cross_kv, (0, 2, 3, 1)).reshape(2, channels, context.shape[2])
        rows, *res_cols, ctx_key, ctx_val = entry('sp', num_bands, images, heads, text_pad, latent, time_emb, own_context, norm_cols, res_time, ctx_w)
        weights = (proj_inout, jnp.transpose(self_qkv, (0, 2, 3, 1)).reshape(3, channels, channels), self_out.reshape(channels, channels), jnp.transpose(cross_q, (1, 2, 0)).reshape(channels, channels), cross_out.reshape(channels, channels), ff_in, ff_out)
        conv_weights = res_conv.reshape(4, 9 * channels, channels)
        before = ()
        for i in range(images):
            rows, before = res_block_in('sp', num_bands, i, images, rows.reshape(tokens, channels), latent, res_cols[0], conv_weights, 0, width, group_width, before)
        stacked, parts = former(*before, attn_cols, ctx_key, ctx_val, weights, text, group_width)
        out = res_block_out('sp', num_bands, stacked, parts, res_cols[1], conv_weights, 2, width, group_width)
        return out.reshape(latent.shape)

    band_spec = P('dp', 'sp', None, None)
    shared = P()
    in_specs = (band_spec, P('dp', None), P('dp', None, None)) + (shared,) * 12
    return jax.shard_map(local_stage, mesh=mesh, in_specs=in_specs, out_specs=band_spec, check_vma=False)
```

time: 337 us -> 312 us (0.926); the launches traced: 332 us -> 312 us
  local copies, waits for them, and re-layouts: 22.7 us -> 8.73 us
  Pallas kernels: 288 us -> 301 us
  starting transfers between devices: 11.9 us -> 0 us
  matrix products: 5.94 us -> 0 us
    pallas_call x2 -> x3, Pallas kernels: 72.9 us -> 102 us  [the longest x2 71.6 us: res_block_in(): pl.pallas_call(functools.partial(res_in_kernel, axis, bands, image, sendi...]
    all_to_all x2 -> x0, starting transfers between devices: 11.9 us -> none  [local_stage(): lax.all_to_all(rows[i * num_bands:(i + 1) * num_bands], 'sp', 0, 1, tiled...]
    pallas_call x1, Pallas kernels: 126 us -> 115 us  [former(): pl.pallas_call(functools.partial(former_kernel, heads, text, group_width,...]
    optimization_barrier x2 -> x0, local copies, waits for them, and re-layouts: 6.44 us -> none  [local_stage(): rows, later = lax.optimization_barrier((rows, later))]
    dot_general x4 -> x0, matrix products: 5.94 us -> none  [the longest x2 3.51 us: time_project(): return jnp.dot(time_act, weight, preferred_element_type=F32)]
    pallas_call x1, Pallas kernels: 89.4 us -> 84.1 us  [res_block_out(): pl.pallas_call(functools.partial(res_out_kernel, axis, bands, width, grou...]
    slice x5 -> x0, local copies, waits for them, and re-layouts: 4.79 us -> none  [the longest x2 4.56 us: local_stage(): rows[i * num_bands:(i + 1) * num_bands]]
    unnamed x20 -> x14, local copies, waits for them, and re-layouts: 4.99 us -> 6.76 us
  transfers between devices with their start and end apart: 2 -> 0, of which waited for: 1 -> 0; matrix products, arithmetic and copies ran while one was open for 6% -> 0% of each run, Pallas kernels for 11% -> 0%
where the time goes in v2:
time: 312 us
  Pallas kernels  301 us (96%)
  local copies, waits for them, and re-layouts  8.73 us (3%)
    pallas_call x1, Pallas kernels, former(): pl.pallas_call(functools.partial(former_kernel, heads, text, group_width,...  115 us
    pallas_call x1, Pallas kernels, res_block_out(): pl.pallas_call(functools.partial(res_out_kernel, axis, bands, width, grou...  84.1 us
    pallas_call x2, Pallas kernels, res_block_in(): pl.pallas_call(functools.partial(res_in_kernel, axis, bands, image, sendi...  71.6 us
    pallas_call x1, Pallas kernels, entry(): pl.pallas_call(functools.partial(entry_kernel, axis, bands), out_shape=(j...  30.3 us
    unnamed x14, local copies, waits for them, and re-layouts  6.76 us

profile of v2, /device:TPU:81, one launch (start us, length us, event | category | flops | bytes accessed | tf_op | source)
XLA Modules:
  0.0 311.8 jit_solution(10524954211232471835)
XLA Ops:
  0.0 0.0 copy-start
  0.0 1.5 copy-done
  1.5 0.5 constant_dynamic-slice_fusion
  2.1 0.8 pad.14.ctx_ref
  2.8 0.9 copy.23
  3.7 0.1 reshape.39
  3.9 0.3 copy.24
  4.2 0.9 convert_bitcast_fusion.norm_ref
  5.0 30.3 %entry.1 = (bf16[8,192,640]{2,1,0:T(8,128)(2,1)}, f32[2,640,8]{2,1,0:T(8,128)}, f32[2,640,8]{2,1,0:T(8,128)}, bf16[2,8,80,128]{3,2,1,0:T(8,128)(2,1)}, bf16[2,640,128]{2,1,0:T(8,128)(2,1)}) custom-call(bf16[16,1,192,640]{3,2,1,0:T(8,128)(2,1)} %refs_0_.2, bf16[16,1280]{1,0:T(8,128)(2,1)} %time_ref.1, bf16[2,128,768]{2,1,0:T(8,128)(2,1)} %pad.14.ctx_ref, ...), custom_call_target="tpu_custom_call" | custom-call | flops 1000000000 | bytes 8388608 | tf_op jit(solution)/shard_map/entry/pallas_call | solution.py:202
  35.4 36.1 %res_in.2 = (bf16[8,192,640]{2,1,0:T(8,128)(2,1)}, bf16[2,640,1536]{2,1,0:T(8,128)(2,1)}, f32[2,640,256]{2,1,0:T(8,128)}) custom-call(bf16[1536,640]{1,0:T(8,128)(2,1)} %bitcast.35, f32[2,640,8]{2,1,0:T(8,128)} %get-tuple-element.18.cols_ref, bf16[4,5760,640]{2,1,0:T(8,128)(2,1)} %bitcast.31, bf16[16,1,192,640]{3,2,1,0:T(8,128)(2,1)} %refs_0_.2), custom_call_target="tpu_custom_call" | custom-call | flops 22649241600 | bytes 16384000 | tf_op jit(solution)/shard_map/res_in/pallas_call | solution.py:357
  71.5 0.0 copy-start.4
  71.5 35.5 %res_in.3 = (bf16[2,640,1536]{2,1,0:T(8,128)(2,1)}, f32[2,640,256]{2,1,0:T(8,128)}) custom-call(bf16[1536,640]{1,0:T(8,128)(2,1)} %bitcast.39, f32[2,640,8]{2,1,0:T(8,128)} %get-tuple-element.18.cols_ref, bf16[4,5760,640]{2,1,0:T(8,128)(2,1)} %bitcast.32, ...), custom_call_target="tpu_custom_call", output_to_operand_aliasing={{0}: (3, {}), {1}: (4, {})} | custom-call | flops 22649241600 | bytes 16384000 | tf_op jit(solution)/shard_map/res_in/pallas_call | solution.py:357
  107.0 0.0 copy-done.4
  107.0 0.1 copy.25
  107.1 0.1 reshape.44
  107.2 0.2 copy.26
  107.4 0.8 convert_bitcast_fusion.1.cols_ref
  108.2 0.0 copy-start.2
  108.2 115.3 %former.1 = (bf16[2,640,1536]{2,1,0:T(8,128)(2,1)}, f32[2,640,256]{2,1,0:T(8,128)}) custom-call(bf16[2,640,1536]{2,1,0:T(8,128)(2,1)} %get-tuple-element.22.hid_ref, f32[2,640,256]{2,1,0:T(8,128)} %get-tuple-element.23.part_in_ref, f32[640,8]{1,0:T(8,128)} %convert_bitcast_fusion.1.cols_ref, bf16[2,8,80,128]{3,2,1,0:T(8,128)(2,1)} %get-tuple-element.24.ctx_key_ref, ...), custom_call_target="tpu_custom_call" | custom-call | flops 86570434560 | bytes 62914560 | tf_op jit(solution)/shard_map/former/pallas_call | solution.py:557
  223.5 0.0 copy-done.2
  223.5 0.0 copy-start.3
  223.5 1.3 copy-done.3
  224.8 84.1 %res_out.1 = bf16[16,192,640]{2,1,0:T(8,128)(2,1)S(1)} custom-call(bf16[2,640,1536]{2,1,0:T(8,128)(2,1)} %get-tuple-element.26.hid_hbm, f32[2,640,256]{2,1,0:T(8,128)S(1)} %copy-done.3, f32[2,640,8]{2,1,0:T(8,128)S(1)} %copy-done.2, bf16[4,5760,640]{2,1,0:T(8,128)(2,1)} %bitcast.33), custom_call_target="tpu_custom_call" | custom-call | flops 45298483200 | bytes 16384000 | tf_op jit(solution)/shard_map/res_out/pallas_call | solution.py:379
  309.0 0.0 copy-start.1
  309.0 2.0 copy.34
  311.0 0.9 copy-done.1
  (1 shorter events, 0.0 us)
Async XLA Ops:
  0.0 1.5 copy-start
  71.5 35.5 %copy-start.4 = (bf16[2,32,20]{1,0,2:T(2,128)(2,1)S(1)}, bf16[2,32,20]{1,0,2:T(2,128)(2,1)}, u32[]{:S(2)}) copy-start(bf16[2,32,20]{1,0,2:T(2,128)(2,1)} %param.21) | copy-start | bytes 7684
  108.2 115.3 %copy-start.2 = (f32[2,640,8]{2,1,0:T(8,128)S(1)}, f32[2,640,8]{2,1,0:T(8,128)}, u32[]{:S(2)}) copy-start(f32[2,640,8]{2,1,0:T(8,128)} %get-tuple-element.28.cols_ref) | copy-start | bytes 122884
  223.5 1.3 copy-start.3
  309.0 2.9 copy-start.1
